TPU v7x, 32 devices: a whole 2x2x4 slice. The times are simulated.
32 devices in a mesh: dp: 8 (over z, x), tensor: 4 (over y, core).
Axes of the slice: x: 2, y: 2, z: 4, core: 2. Of those that a mesh axis runs over, the one named last changes fastest.
Arguments:
- inputs: bfloat16 [8, 2048, 768], P('dp', 'tensor'), may hold values from -6 to 6
- segments: int32 [8, 2048], P('dp', 'tensor'), may hold values from 0 to 7, never falling along the last dimension, each value on 1 to 1792 neighbouring positions
- query_weight: bfloat16 [768, 768], P('dp', 'tensor'), may hold values from -0.21875 to 0.21875
- query_bias: bfloat16 [768], P('tensor'), may hold values from -1.75 to 1.75
- key_weight: bfloat16 [768, 768], P('dp', 'tensor'), may hold values from -0.21875 to 0.21875
- value_weight: bfloat16 [768, 768], P('dp', 'tensor'), may hold values from -0.21875 to 0.21875
- value_bias: bfloat16 [768], P('tensor'), may hold values from -1.75 to 1.75
- output_weight: bfloat16 [768, 768], P('tensor', 'dp'), may hold values from -0.875 to 0.875
- output_bias: bfloat16 [768], replicated, may hold values from -1.75 to 1.75
- up_weight: bfloat16 [768, 3072], P('dp', 'tensor'), may hold values from -0.21875 to 0.21875
- up_bias: bfloat16 [3072], P('tensor'), may hold values from -1.75 to 1.75
- down_weight: bfloat16 [3072, 768], P('tensor', 'dp'), may hold values from -0.109375 to 0.109375
- down_bias: bfloat16 [768], replicated, may hold values from -1.75 to 1.75
- first_gain: float32 [768], replicated, may hold values from 0.5 to 1.5
- first_shift: float32 [768], replicated, may hold values from -1.75 to 1.75
- second_gain: float32 [768], replicated, may hold values from 0.5 to 1.5
- second_shift: float32 [768], replicated, may hold values from -1.75 to 1.75
- cotangent: bfloat16 [8, 2048, 768], P('dp', 'tensor'), may hold values from -6 to 6
Outputs:
- layer_out: bfloat16 [8, 2048, 768], P('dp', 'tensor')
- grad_inputs: float32 [8, 2048, 768], P('dp', 'tensor')
- query_weight_gradient: float32 [768, 768], P('dp', 'tensor')
- sum_query: float32 [768], P('tensor')
- key_weight_gradient: float32 [768, 768], P('dp', 'tensor')
- value_weight_gradient: float32 [768, 768], P('dp', 'tensor')
- sum_value: float32 [768], P('tensor')
- grad_output: float32 [768, 768], P('tensor', 'dp')
- sum_output: float32 [768], replicated
- up_weight_gradient: float32 [768, 3072], P('dp', 'tensor')
- sum_up: float32 [3072], P('tensor')
- down_weight_gradient: float32 [3072, 768], P('tensor', 'dp')
- sum_down: float32 [768], replicated
- gain_first: float32 [768], replicated
- shift_first: float32 [768], replicated
- gain_second: float32 [768], replicated
- shift_second: float32 [768], replicated
Inputs may be any that keep to these rules, and one draw needn't show every extreme that they name: `segments`: document numbers never fall along a sequence; each document has 1 to 1792 tokens, and one has exactly 1792.
All inputs are finite; a program needn't handle non-finite values.
Results may differ from a plain program's by a relative error of at most 0.014.
Values may be sent and summed in bfloat16 or wider, within the bound.
No kernel may reach another device: no remote copies, remote signals or barrier semaphores. Data moves between devices by JAX's collectives and lax.ppermute only.
A program may use at most 128 MiB of HBM per device.

v0:
```python
import jax
import jax.numpy as jnp
from jax import lax
from jax.sharding import PartitionSpec as P

HEAD = 64
FF = 3072


eps_norm = 1e-12
root_half = 0.7071067811865476
density = 0.3989422804014327


def product(left, right):
    return jnp.dot(left, right, preferred_element_type=jnp.float32)


def column_sum(values):
    return jnp.sum(values, axis=(0, 1))


def normalize(values, gain, offset):
    average = jnp.mean(values, axis=-1, keepdims=True)
    centred = values - average
    inverse = lax.rsqrt(jnp.mean(centred * centred, axis=-1, keepdims=True) + eps_norm)
    normed = centred * inverse
    return (normed * gain + offset, normed, inverse)


def norm_back(upstream, normed, inverse, gain):
    scaled = upstream * gain
    centred = scaled - jnp.mean(scaled, axis=-1, keepdims=True)
    return (centred - normed * jnp.mean(scaled * normed, axis=-1, keepdims=True)) * inverse


def gelu_value(inner):
    return inner * 0.5 * (1.0 + lax.erf(inner * root_half))


def gelu_slope(inner):
    return 0.5 * (1.0 + lax.erf(inner * root_half)) + inner * density * jnp.exp(
        -0.5 * inner * inner
    )


def block_pieces(position, blocks, block_rows, queries, keys_all, values_all, doc_ids):
    sequence = position // blocks
    offset = position % blocks * block_rows
    seq_queries = lax.dynamic_index_in_dim(queries, sequence, 0, keepdims=False)
    seq_keys = lax.dynamic_index_in_dim(keys_all, sequence, 0, keepdims=False)
    seq_values = lax.dynamic_index_in_dim(values_all, sequence, 0, keepdims=False)
    seq_docs = lax.dynamic_index_in_dim(doc_ids, sequence, 0, keepdims=False)
    block_queries = lax.dynamic_slice_in_dim(seq_queries, offset, block_rows, 0)
    block_docs = lax.dynamic_slice_in_dim(seq_docs, offset, block_rows, 0)
    scores = (
        jnp.einsum("qhd,khd->hqk", block_queries, seq_keys, preferred_element_type=jnp.float32)
        * 0.125
    )
    same_doc = block_docs[:, None] == seq_docs[None, :]
    masked = jnp.where(same_doc[None], scores, -1e30)
    return (sequence, offset, block_queries, seq_keys, seq_values, masked)


def attend_forward(queries, keys_all, values_all, doc_ids):
    sequences, length, head_count, head_size = queries.shape
    block_rows = min(512, length)
    blocks = length // block_rows

    def one_block(position):
        pieces = block_pieces(position, blocks, block_rows, queries, keys_all, values_all, doc_ids)
        masked = pieces[5]
        highest = jnp.max(masked, axis=-1, keepdims=True)
        raised = jnp.exp(masked - highest)
        totals = jnp.sum(raised, axis=-1, keepdims=True)
        weights = (raised / totals).astype(jnp.bfloat16)
        mixed = jnp.einsum("hqk,khd->qhd", weights, pieces[4], preferred_element_type=jnp.float32)
        return (mixed, highest[..., 0] + jnp.log(totals[..., 0]))

    mixed, log_total = lax.map(one_block, jnp.arange(sequences * blocks, dtype=jnp.int32))
    return (mixed.reshape(sequences, length, head_count * head_size), log_total)


def attend_back(queries, keys_all, values_all, doc_ids, upstream, log_total):
    sequences, length, head_count, head_size = queries.shape
    block_rows = min(512, length)
    blocks = length // block_rows
    anchor = jnp.int32(0)

    def one_block(position, carry):
        grad_queries, grad_keys, grad_values = carry
        pieces = block_pieces(position, blocks, block_rows, queries, keys_all, values_all, doc_ids)
        sequence, offset, block_queries, seq_keys, seq_values, masked = pieces
        seq_upstream = lax.dynamic_index_in_dim(upstream, sequence, 0, keepdims=False)
        block_upstream = lax.dynamic_slice_in_dim(seq_upstream, offset, block_rows, 0)
        block_total = lax.dynamic_index_in_dim(log_total, position, 0, keepdims=False)
        weights = jnp.exp(masked - block_total[:, :, None])
        grad_weights = jnp.einsum(
            "qhd,khd->hqk", block_upstream, seq_values, preferred_element_type=jnp.float32
        )
        inner = jnp.sum(weights * grad_weights, axis=-1, keepdims=True)
        grad_scores = (weights * (grad_weights - inner)).astype(jnp.bfloat16)
        block_grad = (
            jnp.einsum("hqk,khd->qhd", grad_scores, seq_keys, preferred_element_type=jnp.float32)
            * 0.125
        )
        add_keys = (
            jnp.einsum(
                "hqk,qhd->khd", grad_scores, block_queries, preferred_element_type=jnp.float32
            )
            * 0.125
        )
        add_values = jnp.einsum(
            "hqk,qhd->khd",
            weights.astype(jnp.bfloat16),
            block_upstream,
            preferred_element_type=jnp.float32,
        )
        grad_queries = lax.dynamic_update_slice(
            grad_queries, block_grad[None], (sequence, offset, anchor, anchor)
        )
        old_keys = lax.dynamic_index_in_dim(grad_keys, sequence, 0, keepdims=True)
        grad_keys = old_keys + add_keys[None]
        old_values = lax.dynamic_index_in_dim(grad_values, sequence, 0, keepdims=True)
        grad_values = old_values + add_values[None]
        return (grad_queries, grad_keys, grad_values)

    empty = jnp.zeros(queries.shape, jnp.float32)
    return lax.fori_loop(0, sequences * blocks, one_block, (empty, empty, empty))


def local(
    inputs,
    segments,
    query_weight,
    query_bias,
    key_weight,
    value_weight,
    value_bias,
    output_weight,
    output_bias,
    up_weight,
    up_bias,
    down_weight,
    down_bias,
    first_gain,
    first_shift,
    second_gain,
    second_shift,
    cotangent,
):
    gathered = (
        lax.all_gather(query_weight, "dp", axis=0, tiled=True),
        lax.all_gather(key_weight, "dp", axis=0, tiled=True),
        lax.all_gather(value_weight, "dp", axis=0, tiled=True),
        lax.all_gather(up_weight, "dp", axis=0, tiled=True),
        lax.all_gather(output_weight, "dp", axis=1, tiled=True),
        lax.all_gather(down_weight, "dp", axis=1, tiled=True),
    )
    (
        complete_query_weight,
        complete_key_weight,
        complete_value_weight,
        complete_up_weight,
        complete_output_weight,
        complete_down_weight,
    ) = gathered
    gathered_token_rows = lax.all_gather(inputs, "tensor", axis=1, tiled=True)
    docs_all = lax.all_gather(segments, "tensor", axis=1, tiled=True)
    sequences, length, width = gathered_token_rows.shape
    head_count = complete_query_weight.shape[1] // HEAD
    shaped = (sequences, length, head_count, HEAD)
    flat = (sequences, length, head_count * HEAD)
    queries = (
        (product(gathered_token_rows, complete_query_weight) + query_bias)
        .astype(jnp.bfloat16)
        .reshape(shaped)
    )
    keys_all = (
        product(gathered_token_rows, complete_key_weight).astype(jnp.bfloat16).reshape(shaped)
    )
    values_all = (
        (product(gathered_token_rows, complete_value_weight) + value_bias)
        .astype(jnp.bfloat16)
        .reshape(shaped)
    )
    mixed, log_total = attend_forward(queries, keys_all, values_all, docs_all)
    mixed_reduced_precision = mixed.astype(jnp.bfloat16)
    attn_sum = lax.psum_scatter(
        product(mixed_reduced_precision, complete_output_weight),
        "tensor",
        scatter_dimension=1,
        tiled=True,
    )
    hidden = inputs.astype(jnp.float32) + attn_sum + output_bias
    normed_first, unit_first, inverse_first = normalize(hidden, first_gain, first_shift)
    first_low = normed_first.astype(jnp.bfloat16)
    feedforward_rows = lax.all_gather(first_low, "tensor", axis=1, tiled=True)
    inner = product(feedforward_rows, complete_up_weight) + up_bias
    gelu_activation_out = gelu_value(inner).astype(jnp.bfloat16)
    ffn_part = product(gelu_activation_out, complete_down_weight)
    ffn_sum = lax.psum_scatter(ffn_part, "tensor", scatter_dimension=1, tiled=True)
    second_in = normed_first + ffn_sum + down_bias
    layer_out, unit_second, inverse_second = normalize(second_in, second_gain, second_shift)
    upstream = cotangent.astype(jnp.float32)
    grad_second = norm_back(upstream, unit_second, inverse_second, second_gain)
    gain_second = column_sum(upstream * unit_second)
    shift_second = column_sum(upstream)
    sum_down = column_sum(grad_second)
    second_low = grad_second.astype(jnp.bfloat16)
    feedforward_gradient = lax.all_gather(second_low, "tensor", axis=1, tiled=True)
    activation_gradient = jnp.einsum(
        "znj,aj->zna",
        feedforward_gradient,
        complete_down_weight,
        preferred_element_type=jnp.float32,
    )
    inner_hidden_gradient = (activation_gradient * gelu_slope(inner)).astype(jnp.bfloat16)
    down_weight_gradient = jnp.einsum(
        "rhc,rhi->ci", gelu_activation_out, feedforward_gradient, preferred_element_type=jnp.float32
    )
    up_weight_gradient = jnp.einsum(
        "jkg,jkp->gp", feedforward_rows, inner_hidden_gradient, preferred_element_type=jnp.float32
    )
    sum_up = column_sum(inner_hidden_gradient.astype(jnp.float32))
    backward_portion = jnp.einsum(
        "ght,xt->ghx", inner_hidden_gradient, complete_up_weight, preferred_element_type=jnp.float32
    )
    back_sum = lax.psum_scatter(backward_portion, "tensor", scatter_dimension=1, tiled=True)
    grad_first = grad_second + back_sum
    grad_hidden = norm_back(grad_first, unit_first, inverse_first, first_gain)
    gain_first = column_sum(grad_first * unit_first)
    shift_first = column_sum(grad_first)
    sum_output = column_sum(grad_hidden)
    attention_gradient = lax.all_gather(
        grad_hidden.astype(jnp.bfloat16), "tensor", axis=1, tiled=True
    )
    grad_mixed = jnp.einsum(
        "uwa,xa->uwx",
        attention_gradient,
        complete_output_weight,
        preferred_element_type=jnp.float32,
    ).astype(jnp.bfloat16)
    grad_output = jnp.einsum(
        "qub,qun->bn",
        mixed_reduced_precision,
        attention_gradient,
        preferred_element_type=jnp.float32,
    )
    grad_queries, grad_keys, grad_values = attend_back(
        queries, keys_all, values_all, docs_all, grad_mixed.reshape(shaped), log_total
    )
    query_reduced_precision = grad_queries.astype(jnp.bfloat16).reshape(flat)
    key_reduced_precision = grad_keys.astype(jnp.bfloat16).reshape(flat)
    value_reduced_precision = grad_values.astype(jnp.bfloat16).reshape(flat)
    query_weight_gradient = jnp.einsum(
        "mwj,mwb->jb",
        gathered_token_rows,
        query_reduced_precision,
        preferred_element_type=jnp.float32,
    )
    key_weight_gradient = jnp.einsum(
        "mwj,mwb->jb",
        gathered_token_rows,
        key_reduced_precision,
        preferred_element_type=jnp.float32,
    )
    value_weight_gradient = jnp.einsum(
        "mwj,mwb->jb",
        gathered_token_rows,
        value_reduced_precision,
        preferred_element_type=jnp.float32,
    )
    sum_query = column_sum(query_reduced_precision.astype(jnp.float32))
    sum_value = column_sum(value_reduced_precision.astype(jnp.float32))
    backward_token_rows = jnp.einsum(
        "oia,ka->oik",
        query_reduced_precision,
        complete_query_weight,
        preferred_element_type=jnp.float32,
    )
    backward_token_rows = backward_token_rows + jnp.einsum(
        "oia,ka->oik",
        key_reduced_precision,
        complete_key_weight,
        preferred_element_type=jnp.float32,
    )
    backward_token_rows = backward_token_rows + jnp.einsum(
        "oia,ka->oik",
        value_reduced_precision,
        complete_value_weight,
        preferred_element_type=jnp.float32,
    )
    grad_inputs = grad_hidden + lax.psum_scatter(
        backward_token_rows.astype(jnp.bfloat16), "tensor", scatter_dimension=1, tiled=True
    ).astype(jnp.float32)
    owned = (
        lax.psum_scatter(query_weight_gradient, "dp", scatter_dimension=0, tiled=True),
        lax.psum_scatter(key_weight_gradient, "dp", scatter_dimension=0, tiled=True),
        lax.psum_scatter(value_weight_gradient, "dp", scatter_dimension=0, tiled=True),
        lax.psum_scatter(up_weight_gradient, "dp", scatter_dimension=0, tiled=True),
        lax.psum_scatter(grad_output, "dp", scatter_dimension=1, tiled=True),
        lax.psum_scatter(down_weight_gradient, "dp", scatter_dimension=1, tiled=True),
    )
    slot = lax.axis_index("tensor")
    head_width = sum_query.shape[0]
    unit_width = FF // lax.axis_size("tensor")
    place_query = lax.dynamic_update_slice(
        jnp.zeros((width,), jnp.float32), sum_query, (slot * head_width,)
    )
    place_value = lax.dynamic_update_slice(
        jnp.zeros((width,), jnp.float32), sum_value, (slot * head_width,)
    )
    place_up = lax.dynamic_update_slice(jnp.zeros((FF,), jnp.float32), sum_up, (slot * unit_width,))
    totals = lax.psum(
        (
            place_query,
            place_value,
            place_up,
            sum_output,
            sum_down,
            gain_first,
            shift_first,
            gain_second,
            shift_second,
        ),
        ("dp", "tensor"),
    )
    query_share = lax.dynamic_slice_in_dim(totals[0], slot * head_width, head_width)
    value_share = lax.dynamic_slice_in_dim(totals[1], slot * head_width, head_width)
    up_share = lax.dynamic_slice_in_dim(totals[2], slot * unit_width, unit_width)
    return (
        layer_out.astype(jnp.bfloat16),
        grad_inputs,
        owned[0],
        query_share,
        owned[1],
        owned[2],
        value_share,
        owned[4],
        totals[3],
        owned[3],
        up_share,
        owned[5],
        totals[4],
        totals[5],
        totals[6],
        totals[7],
        totals[8],
    )


def solution(mesh):
    return jax.shard_map(
        local,
        mesh=mesh,
        in_specs=(
            P("dp", "tensor", None),
            P("dp", "tensor"),
            P("dp", "tensor"),
            P("tensor"),
            P("dp", "tensor"),
            P("dp", "tensor"),
            P("tensor"),
            P("tensor", "dp"),
            P(),
            P("dp", "tensor"),
            P("tensor"),
            P("tensor", "dp"),
            P(),
            P(),
            P(),
            P(),
            P(),
            P("dp", "tensor", None),
        ),
        out_specs=(
            P("dp", "tensor", None),
            P("dp", "tensor", None),
            P("dp", "tensor"),
            P("tensor"),
            P("dp", "tensor"),
            P("dp", "tensor"),
            P("tensor"),
            P("tensor", "dp"),
            P(),
            P("dp", "tensor"),
            P("tensor"),
            P("tensor", "dp"),
            P(),
            P(),
            P(),
            P(),
            P(),
        ),
        check_vma=False,
    )
```

profile of v0, /device:TPU:0, one launch (start us, length us, event | category | flops | bytes accessed | tf_op | source)
XLA Modules:
  0.0 1198.1 jit_solution(2556542930120065945)
XLA Ops:
  11.0 6.4 all_gather.33
  17.4 31.9 %all_gather.38 = bf16[192,768]{0,1:T(8,128)(2,1)S(1)} all-gather(bf16[192,96]{0,1:T(8,128)(2,1)S(1)} %copy.43), channel_id=1, replica_groups=mesh['dp'=8,'tensor'=4] {'dp'}, dimensions={1}, use_global_device_ids=true | all-gather | bytes 331776 | tf_op jit(solution)/shard_map/all_gather | solution.py:157
  49.3 31.2 %all_gather.35 = bf16[768,192]{1,0:T(8,128)(2,1)S(1)} all-gather(bf16[96,192]{1,0:T(8,128)(2,1)} %param.24), channel_id=1, replica_groups=mesh['dp'=8,'tensor'=4] {'dp'}, dimensions={0}, use_global_device_ids=true | all-gather | bytes 331776 | tf_op jit(solution)/shard_map/all_gather | solution.py:153
  80.6 31.2 %all_gather.36 = bf16[768,192]{1,0:T(8,128)(2,1)S(1)} all-gather(bf16[96,192]{1,0:T(8,128)(2,1)} %param.26), channel_id=1, replica_groups=mesh['dp'=8,'tensor'=4] {'dp'}, dimensions={0}, use_global_device_ids=true | all-gather | bytes 331776 | tf_op jit(solution)/shard_map/all_gather | solution.py:154
  111.8 31.2 %all_gather.37 = bf16[768,192]{1,0:T(8,128)(2,1)S(1)} all-gather(bf16[96,192]{1,0:T(8,128)(2,1)} %param.27), channel_id=1, replica_groups=mesh['dp'=8,'tensor'=4] {'dp'}, dimensions={0}, use_global_device_ids=true | all-gather | bytes 331776 | tf_op jit(solution)/shard_map/all_gather | solution.py:155
  143.0 3.2 fusion.81
  148.6 94.6 %while.34 = (s32[]{:T(128)}, bf16[4,512,3,64]{1,3,2,0:T(8,128)(2,1)}, f32[4,3,512]{2,1,0:T(4,128)}, s32[4]{0:T(128)S(1)}, s32[1,2048]{1,0:T(1,128)S(1)}, /*index...) while((s32[]{:T(128)}, ...), condition=%wide.region_3.4_spmd, body=%wide.region_0.3_spmd.sunk | while | flops 844102144 | bytes 50467196 | solution.py:80
  151.9 6.0 fusion.163
  157.9 6.8 fusion.164
  164.7 6.7 fusion.165
  175.5 6.0 fusion.163
  181.5 6.8 fusion.164
  188.3 6.7 fusion.165
  199.1 6.0 fusion.163
  205.1 6.8 fusion.164
  212.0 6.7 fusion.165
  222.8 6.0 fusion.163
  228.8 6.8 fusion.164
  235.6 6.7 fusion.165
  246.7 3.7 convolution_bitcast_fusion
  251.1 59.4 %reduce-scatter.19.cloned.1.call-done = f32[1,512,768]{2,1,0:T(8,128)} async-done(((f32[1,2048,768]{2,1,0:T(8,128)}), f32[1,512,768]{2,1,0:T(8,128)}) %reduce-scatter.19.cloned.1.call-update) | async-done | bytes 1572880 | tf_op jit(solution)/shard_map/reduce_scatter | solution.py:189
  315.4 27.5 %all-gather.9.cloned.1.call-done = bf16[1,2048,768]{2,1,0:T(8,128)(2,1)} async-done(((bf16[1,512,768]{2,1,0:T(8,128)(2,1)}), bf16[1,2048,768]{2,1,0:T(8,128)(2,1)}) %all-gather.9.cloned.1.call-update) | async-done | bytes 3145744 | tf_op jit(solution)/shard_map/all_gather | solution.py:198
  342.9 6.9 multiply_convert_fusion.1
  349.9 36.6 %all-gather.13.cloned.1.call-done = bf16[768,768]{0,1:T(8,128)(2,1)} async-done(((bf16[768,96]{0,1:T(8,128)(2,1)}), bf16[768,768]{0,1:T(8,128)(2,1)}) %all-gather.13.cloned.1.call-update) | async-done | bytes 1179664 | tf_op jit(solution)/shard_map/all_gather | solution.py:158
  386.4 7.5 convolution_bitcast_fusion.2
  395.2 56.0 %reduce-scatter.21.cloned.1.call-done = f32[1,512,768]{2,1,0:T(8,128)} async-done(((f32[1,2048,768]{2,1,0:T(8,128)}), f32[1,512,768]{2,1,0:T(8,128)}) %reduce-scatter.21.cloned.1.call-update) | async-done | bytes 1572880 | tf_op jit(solution)/shard_map/reduce_scatter | solution.py:202
  459.3 28.6 %all-gather.15.cloned.1.call-done = bf16[1,2048,768]{2,1,0:T(8,128)(2,1)} async-done(((bf16[1,512,768]{2,1,0:T(8,128)(2,1)}), bf16[1,2048,768]{2,1,0:T(8,128)(2,1)}) %all-gather.15.cloned.1.call-update) | async-done | bytes 3145744 | tf_op jit(solution)/shard_map/all_gather | solution.py:211
  487.9 8.1 convert_reduce_fusion
  497.6 4.5 convolution_bitcast_fusion.1
  502.2 58.8 %reduce-scatter.23.cloned.1.call-done = f32[1,512,768]{2,1,0:T(8,128)} async-done(((f32[1,2048,768]{2,1,0:T(8,128)}), f32[1,512,768]{2,1,0:T(8,128)}) %reduce-scatter.23.cloned.1.call-update) | async-done | bytes 1572880 | tf_op jit(solution)/shard_map/reduce_scatter | solution.py:229
  561.0 3.3 multiply_reduce_fusion.1
  567.7 28.6 %all-gather.17.cloned.1.call-done = bf16[1,2048,768]{2,1,0:T(8,128)(2,1)} async-done(((bf16[1,512,768]{2,1,0:T(8,128)(2,1)}), bf16[1,2048,768]{2,1,0:T(8,128)(2,1)}) %all-gather.17.cloned.1.call-update) | async-done | bytes 3145744 | tf_op jit(solution)/shard_map/all_gather | solution.py:235
  596.3 3.1 fusion.84
  600.3 137.5 %while.35 = (s32[]{:T(128)}, bf16[1,2048,3,64]{1,3,2,0:T(8,128)(2,1)}, f32[1,2048,3,64]{1,3,2,0:T(8,128)}, f32[1,2048,3,64]{1,3,2,0:T(8,128)}, s32[1,2048]{1,0:T...) while((s32[]{:T(128)}, ...), condition=%wide.region_17.18_spmd.clone, body=%wide.region_15.17_spmd.clone.sunk | while | flops 2063563264 | bytes 150399440 | solution.py:129
  614.3 4.7 fusion.177
  619.0 5.8 multiply_reduce_fusion.7
  624.7 6.1 multiply_convert_fusion.3
  630.9 5.8 fusion.175
  636.7 3.5 fusion.176
  644.8 6.1 fusion.177
  650.9 5.8 multiply_reduce_fusion.7
  656.6 6.1 multiply_convert_fusion.3
  662.7 5.9 fusion.175
  668.6 4.1 fusion.176
  677.2 6.1 fusion.177
  683.3 5.8 multiply_reduce_fusion.7
  689.1 6.1 multiply_convert_fusion.3
  695.2 5.8 fusion.175
  701.1 4.1 fusion.176
  709.7 6.1 fusion.177
  715.8 5.8 multiply_reduce_fusion.7
  721.6 6.1 multiply_convert_fusion.3
  727.7 5.8 fusion.175
  733.5 4.1 fusion.176
  737.9 4.5 fusion.101
  752.1 6.0 fusion.58
  758.2 7.0 fusion.55
  783.3 40.8 %all-reduce = (f32[768]{0:T(1024)S(1)}, f32[768]{0:T(1024)S(1)}, f32[768]{0:T(1024)}, f32[3072]{0:T(1024)S(1)}, f32[768]{0:T(1024)}, /*index=5*/f32[768]{0:T(1024)}, f32[768]{0:T(1024)}, f32[768]{0:T(1024)}, f32[768]{0:T(1024)}) all-reduce(f32[768]{0:T(1024)S(1)} %dynamic_update_slice.34, ...), channel_id=1, replica_groups=mesh['dp'=8,'tensor'=4] {'dp','tensor'}, use_global_device_ids=true, to_apply=%region_21.22 | all-reduce | flops 9216 | bytes 73728 | tf_op jit(solution)/shard_map/psum | solution.py:315
  827.7 17.3 %reduce-scatter.25.cloned.1.call-done = bf16[1,512,768]{2,1,0:T(8,128)(2,1)} async-done(((bf16[1,2048,768]{2,1,0:T(8,128)(2,1)}), bf16[1,512,768]{2,1,0:T(8,128)(2,1)}) %reduce-scatter.25.cloned.1.call-update) | async-done | bytes 786448 | tf_op jit(solution)/shard_map/reduce_scatter | solution.py:294
  847.4 71.4 %reduce-scatter.27.cloned.1.call-done = f32[96,768]{1,0:T(8,128)} async-done(((f32[768,768]{1,0:T(8,128)}), f32[96,768]{1,0:T(8,128)}) %reduce-scatter.27.cloned.1.call-update) | async-done | bytes 294928 | tf_op jit(solution)/shard_map/reduce_scatter | solution.py:301
  918.8 73.1 %reduce-scatter.29.cloned.1.call-done = f32[768,96]{0,1:T(8,128)} async-done(((f32[768,768]{0,1:T(8,128)}), f32[768,96]{0,1:T(8,128)}) %reduce-scatter.29.cloned.1.call-update) | async-done | bytes 294928 | tf_op jit(solution)/shard_map/reduce_scatter | solution.py:303
  991.9 66.4 %reduce-scatter.35.cloned.1.call-done = f32[96,192]{1,0:T(8,128)} async-done(((f32[768,192]{1,0:T(8,128)}), f32[96,192]{1,0:T(8,128)}) %reduce-scatter.35.cloned.1.call-update) | async-done | bytes 73744
  1058.3 66.1 %reduce-scatter.31.cloned.1.call-done = f32[96,192]{1,0:T(8,128)} async-done(((f32[768,192]{1,0:T(8,128)}), f32[96,192]{1,0:T(8,128)}) %reduce-scatter.31.cloned.1.call-update) | async-done | bytes 73744
  1124.4 66.2 %reduce-scatter.33.cloned.1.call-done = f32[96,192]{1,0:T(8,128)} async-done(((f32[768,192]{1,0:T(8,128)}), f32[96,192]{1,0:T(8,128)}) %reduce-scatter.33.cloned.1.call-update) | async-done | bytes 73744
  (269 shorter events, 89.4 us)
Async XLA Ops:
  8.0 134.9 %all-gather.7.cloned.1.call-start = ((), (), s32[]{:S(2)}) async-start(), calls=%async_computation.10 | async-start | bytes 3932160 | tf_op jit(solution)/shard_map/all_gather | solution.py:168
  8.8 301.7 %reduce-scatter.19.cloned.1.call-start = ((), (), s32[]{:S(2)}) async-start(), calls=%async_computation.11 | async-start | bytes 7864320 | tf_op jit(solution)/shard_map/reduce_scatter | solution.py:189
  80.6 66.9 %copy-start.22 = (bf16[768,192]{1,0:T(8,128)(2,1)}, bf16[768,192]{1,0:T(8,128)(2,1)S(1)}, u32[]{:S(2)}) copy-start(bf16[768,192]{1,0:T(8,128)(2,1)S(1)} %all_gather.35) | copy-start | bytes 884740
  111.8 31.2 %copy-start.18 = (bf16[768,192]{1,0:T(8,128)(2,1)}, bf16[768,192]{1,0:T(8,128)(2,1)S(1)}, u32[]{:S(2)}) copy-start(bf16[768,192]{1,0:T(8,128)(2,1)S(1)} %all_gather.36) | copy-start | bytes 884740
  142.9 3.3 copy-start.24
  157.8 6.8 copy-start.26
  181.5 6.8 copy-start.26
  205.1 6.8 copy-start.26
  228.8 6.8 copy-start.26
  243.2 7.2 copy-start.7
  243.2 7.2 copy-start.15
  250.4 60.1 %copy-start.20 = (bf16[1,512,768]{2,1,0:T(8,128)(2,1)S(1)}, bf16[1,512,768]{2,1,0:T(8,128)(2,1)}, u32[]{:S(2)}) copy-start(bf16[1,512,768]{2,1,0:T(8,128)(2,1)} %param.22) | copy-start | bytes 2359300
  250.4 62.1 %copy-start.28 = (f32[768]{0:T(1024)S(1)}, f32[768]{0:T(1024)}, u32[]{:S(2)}) copy-start(f32[768]{0:T(1024)} %param.35) | copy-start | bytes 9220
  250.4 64.9 %all-gather.11.cloned.1.call-start = ((), (), s32[]{:S(2)}) async-start(), calls=%async_computation.13 | async-start | bytes 1327104 | tf_op jit(solution)/shard_map/all_gather | solution.py:156
  251.0 91.9 %all-gather.9.cloned.1.call-start = ((), (), s32[]{:S(2)}) async-start(), calls=%async_computation.12 | async-start | bytes 3932160 | tf_op jit(solution)/shard_map/all_gather | solution.py:198
  312.5 37.4 %copy-start.29 = (f32[512]{0:T(512)}, f32[512]{0:T(512)S(1)}, u32[]{:S(2)}) copy-start(f32[512]{0:T(512)S(1)} %add_rsqrt_fusion.1) | copy-start | bytes 6148
  314.4 72.0 %all-gather.13.cloned.1.call-start = ((), (), s32[]{:S(2)}) async-start(), calls=%async_computation.14 | async-start | bytes 1327104 | tf_op jit(solution)/shard_map/all_gather | solution.py:158
  315.0 136.1 %reduce-scatter.21.cloned.1.call-start = ((), (), s32[]{:S(2)}) async-start(), calls=%async_computation.15 | async-start | bytes 7864320 | tf_op jit(solution)/shard_map/reduce_scatter | solution.py:202
  315.3 34.5 %copy-start.38 = (f32[768]{0:T(1024)}, f32[768]{0:T(1024)S(1)}, u32[]{:S(2)}) copy-start(f32[768]{0:T(1024)S(1)} %convert_element_type.138) | copy-start | bytes 9220
  393.9 94.0 %all-gather.15.cloned.1.call-start = ((), (), s32[]{:S(2)}) async-start(), calls=%async_computation.16 | async-start | bytes 3932160 | tf_op jit(solution)/shard_map/all_gather | solution.py:211
  395.2 58.3 %copy-start.21 = (bf16[1,512,768]{2,1,0:T(8,128)(2,1)S(1)}, bf16[1,512,768]{2,1,0:T(8,128)(2,1)}, u32[]{:S(2)}) copy-start(bf16[1,512,768]{2,1,0:T(8,128)(2,1)} %param.39) | copy-start | bytes 2359300
  457.1 30.8 %copy-start.39 = (f32[768]{0:T(1024)S(1)}, f32[768]{0:T(1024)}, u32[]{:S(2)}) copy-start(f32[768]{0:T(1024)} %copy-done.38) | copy-start | bytes 9220
  459.2 101.8 %reduce-scatter.23.cloned.1.call-start = ((), (), s32[]{:S(2)}) async-start(), calls=%async_computation.17 | async-start | bytes 7864320 | tf_op jit(solution)/shard_map/reduce_scatter | solution.py:229
  487.9 9.7 copy-start.46
  502.2 58.9 %copy-start.30 = (f32[512]{0:T(512)S(1)}, f32[512]{0:T(512)}, u32[]{:S(2)}) copy-start(f32[512]{0:T(512)} %copy-done.29) | copy-start | bytes 6148
  502.2 94.1 %all-gather.17.cloned.1.call-start = ((), (), s32[]{:S(2)}) async-start(), calls=%async_computation.18 | async-start | bytes 3932160 | tf_op jit(solution)/shard_map/all_gather | solution.py:235
  567.6 258.5 %reduce-scatter.37.cloned.1.call-start = ((), (), s32[]{:S(2)}) async-start(), calls=%async_computation.25 | async-start | bytes 884736
  609.8 4.5 copy-start.2
  609.8 4.5 copy-start.16
  630.9 5.9 copy-start
  636.7 3.6 copy-start.3
  636.7 3.6 copy-start.17
  640.3 4.5 copy-start.2
  640.3 4.5 copy-start.16
  662.7 5.9 copy-start
  668.6 4.1 copy-start.3
  668.6 4.1 copy-start.17
  672.7 4.5 copy-start.2
  672.7 4.5 copy-start.16
  695.2 5.9 copy-start
  701.1 4.1 copy-start.3
  701.1 4.1 copy-start.17
  705.2 4.5 copy-start.2
  705.2 4.5 copy-start.16
  727.7 5.8 copy-start
  733.5 4.1 copy-start.3
  733.5 4.1 copy-start.17
  737.8 4.6 copy-start.4
  737.9 5.6 copy-start.19
  742.4 102.6 %reduce-scatter.25.cloned.1.call-start = ((), (), s32[]{:S(2)}) async-start(), calls=%async_computation.19 | async-start | bytes 3932160 | tf_op jit(solution)/shard_map/reduce_scatter | solution.py:294
  750.3 168.5 %reduce-scatter.27.cloned.1.call-start = ((), (), s32[]{:S(2)}) async-start(), calls=%async_computation.20 | async-start | bytes 2654208 | tf_op jit(solution)/shard_map/reduce_scatter | solution.py:301
  758.2 7.2 copy-start.6
  758.2 233.7 %reduce-scatter.29.cloned.1.call-start = ((), (), s32[]{:S(2)}) async-start(), calls=%async_computation.21 | async-start | bytes 2654208 | tf_op jit(solution)/shard_map/reduce_scatter | solution.py:303
  765.3 293.0 %reduce-scatter.35.cloned.1.call-start = ((), (), s32[]{:S(2)}) async-start(), calls=%async_computation.24 | async-start | bytes 884736
  770.4 354.0 %reduce-scatter.31.cloned.1.call-start = ((), (), s32[]{:S(2)}) async-start(), calls=%async_computation.22 | async-start | bytes 884736
  775.4 5.6 copy-start.40
  775.5 7.8 copy-start.31
  775.5 7.8 copy-start.32
  775.5 7.8 copy-start.33
  775.5 7.8 copy-start.35
  775.5 7.8 copy-start.36
  775.5 7.8 copy-start.37
  775.5 415.0 %reduce-scatter.33.cloned.1.call-start = ((), (), s32[]{:S(2)}) async-start(), calls=%async_computation.23 | async-start | bytes 884736
  778.6 66.4 %copy-start.10 = (f32[1,512,768]{2,1,0:T(8,128)S(1)}, f32[1,512,768]{2,1,0:T(8,128)}, u32[]{:S(2)}) copy-start(f32[1,512,768]{2,1,0:T(8,128)} %copy-done.9) | copy-start | bytes 4718596
  (24 other events, 41.9 us)
Sparse Core Ops, SparseCore 0:
  10.4 31.2 all-gather.6
  250.5 59.8 reduce-scatter.18
  459.4 28.5 all-gather.14
  567.7 28.5 all-gather.16
Sparse Core Ops, SparseCore 1:
  253.1 42.3 all-gather.10
  314.5 28.4 all-gather.8
  345.0 41.4 all-gather.12
  394.0 57.1 reduce-scatter.20
  502.3 58.7 reduce-scatter.22
  742.5 63.4 reduce-scatter.36
  808.3 36.6 reduce-scatter.24
  848.9 69.8 reduce-scatter.26
  922.7 69.1 reduce-scatter.28
  995.8 62.4 reduce-scatter.34
  1062.0 62.3 reduce-scatter.30
  1128.3 62.3 reduce-scatter.32
where the time goes:
time: 1210 us; the launch traced here: 1200 us
  waiting for transfers between devices  658 us (54%)
  matrix products  218 us (18%)
  blocking collectives  173 us (14%)
  other arithmetic  83.3 us (7%)
  local copies, waits for them, and re-layouts  30.5 us (3%)
  loops' own time  18 us (1%)
  between operations  16.3 us (1%)
    unnamed x20, waiting for transfers between devices  201 us
    reduce_scatter x1, waiting for transfers between devices, local(): lax.psum_scatter(down_weight_gradient, 'dp', scatter_dimension=1, tiled=T...  73.1 us
    reduce_scatter x1, waiting for transfers between devices, local(): lax.psum_scatter(up_weight_gradient, 'dp', scatter_dimension=0, tiled=True)  71.4 us
    reduce_scatter x1, waiting for transfers between devices, local(): lax.psum_scatter(product(mixed_reduced_precision, complete_output_weight)...  59.4 us
    reduce_scatter x1, waiting for transfers between devices, local(): lax.psum_scatter(backward_portion, 'tensor', scatter_dimension=1, tiled=T...  58.8 us
    reduce_scatter x1, waiting for transfers between devices, local(): lax.psum_scatter(ffn_part, 'tensor', scatter_dimension=1, tiled=True)  56 us
    psum x1, blocking collectives, local(): lax.psum((place_query, place_value, place_up, sum_output, sum_down, gain_...  40.8 us
    all_gather x1, waiting for transfers between devices, local(): lax.all_gather(down_weight, 'dp', axis=1, tiled=True)  36.6 us
  transfers between devices with their start and end apart: 16, of which 13 were waited for; matrix products, arithmetic and copies ran while one was open for 5% of the time, Pallas kernels for 0%

commit v1 on v0

v1 whole, which is shorter than its diff:
```python
import functools

import jax
import jax.numpy as jnp
from jax import lax
from jax.experimental import pallas as pl
from jax.experimental.pallas import tpu as pltpu
from jax.sharding import PartitionSpec as P

HEAD = 64
BF = jnp.bfloat16
F32 = jnp.float32

eps_norm = 1e-12
root_half = 0.7071067811865476
density = 0.3989422804014327
scale = 0.125
log2e = 1.4426950408889634
far = 1e30
vmem_bytes = 60 * 1024 * 1024


def product(left, right):
    return jnp.dot(left, right, preferred_element_type=F32)


def product_nt(left, right):
    return lax.dot_general(
        left, right, (((1,), (1,)), ((), ())), preferred_element_type=F32
    )


def product_tn(left, right):
    return lax.dot_general(
        left, right, (((0,), (0,)), ((), ())), preferred_element_type=F32
    )


def normalize(values, gain, offset):
    average = jnp.mean(values, axis=-1, keepdims=True)
    centred = values - average
    inverse = lax.rsqrt(jnp.mean(centred * centred, axis=-1, keepdims=True) + eps_norm)
    normed = centred * inverse
    return (normed * gain + offset, normed, inverse)


def norm_back(upstream, normed, inverse, gain):
    scaled = upstream * gain
    centred = scaled - jnp.mean(scaled, axis=-1, keepdims=True)
    return (centred - normed * jnp.mean(scaled * normed, axis=-1, keepdims=True)) * inverse


def load_keys(quarters, aux_key_ref, heads, first, keys_ref):
    width = heads * HEAD
    rows = quarters[0].shape[0]
    for h in range(heads):
        for r, ref in enumerate(quarters):
            block = pl.ds(r * rows, rows)
            keys_ref[h, block, :] = jnp.concatenate(
                [ref[:, first * width + h * HEAD : first * width + (h + 1) * HEAD], aux_key_ref[block, :]],
                axis=1,
            )


def forward_body(heads, *refs):
    quarters, (aux_query_ref, aux_key_ref, query_refs) = refs[:4], (refs[4], refs[5], refs[6:8])
    mixed_ref, log_ref = refs[8:10]
    keys_ref, query_ref, values_ref, out_ref = refs[10:]
    rows = quarters[0].shape[0]
    load_keys(quarters, aux_key_ref, heads, 1, keys_ref)
    width = heads * HEAD
    for h in range(heads):
        for r, ref in enumerate(quarters):
            piece = ref[:, 2 * width + h * HEAD : 2 * width + (h + 1) * HEAD]
            values_ref[h, :, r * rows : (r + 1) * rows] = piece.T
        for r, ref in enumerate(query_refs):
            block = pl.ds(r * rows, rows)
            query_ref[h, block, :] = jnp.concatenate(
                [ref[:, h * HEAD : (h + 1) * HEAD], aux_query_ref[block, :]], axis=1
            )

    def one_head(h, carry):
        scores = product_nt(keys_ref[h], query_ref[h])
        highest = jnp.max(scores, axis=0, keepdims=True)
        raised = jnp.exp2((scores - highest) * (scale * log2e))
        totals = jnp.sum(raised, axis=0, keepdims=True)
        out_ref[h] = product(values_ref[h], raised.astype(BF)) / totals
        log_ref[h] = highest * (scale * log2e) + jnp.log2(totals)
        return carry

    lax.fori_loop(0, heads, one_head, 0)
    for h in range(heads):
        mixed_ref[:, h * HEAD : (h + 1) * HEAD] = out_ref[h].T.astype(BF)


def attend_forward(quarters, aux_query, aux_key, which):
    rows = quarters[0].shape[0]
    length = 4 * rows
    heads = quarters[0].shape[1] // (3 * HEAD)
    count = 2 * rows
    whole = pl.BlockSpec(memory_space=pltpu.VMEM)
    flops = 4 * heads * count * length * HEAD * 4
    return pl.pallas_call(
        functools.partial(forward_body, heads),
        in_specs=[whole] * 8,
        out_specs=[whole] * 2,
        out_shape=[
            jax.ShapeDtypeStruct((count, heads * HEAD), BF),
            jax.ShapeDtypeStruct((heads, 1, count), F32),
        ],
        scratch_shapes=[
            pltpu.VMEM((heads, length, 2 * HEAD), BF),
            pltpu.VMEM((heads, count, 2 * HEAD), BF),
            pltpu.VMEM((heads, HEAD, length), BF),
            pltpu.VMEM((heads, HEAD, count), F32),
        ],
        compiler_params=pltpu.CompilerParams(vmem_limit_bytes=vmem_bytes),
        cost_estimate=pl.CostEstimate(
            flops=flops, bytes_accessed=8 * length * 576, transcendentals=heads * count * length
        ),
        name="attend_forward",
    )(*quarters, aux_query, aux_key, quarters[which[0]], quarters[which[1]])


def backward_body(heads, *refs):
    quarters, (aux_query_ref, aux_key_ref) = refs[:4], refs[4:6]
    mixed_refs, log_refs, grad_refs = refs[6:8], refs[8:10], refs[10:14]
    result_ref = refs[14]
    keys_ref, query_ref, values_ref, up_ref, keys_flat_ref, delta_ref, dq_ref, dk_ref, dv_ref = refs[15:]
    rows = quarters[0].shape[0]
    half = 2 * rows
    width = heads * HEAD
    load_keys(quarters, aux_key_ref, heads, 1, keys_ref)
    load_keys(quarters, aux_query_ref, heads, 0, query_ref)
    for h in range(heads):
        lanes = slice(h * HEAD, (h + 1) * HEAD)
        for r, ref in enumerate(quarters):
            block = pl.ds(r * rows, rows)
            values_ref[h, block, :] = ref[:, 2 * width + h * HEAD : 2 * width + (h + 1) * HEAD]
            keys_flat_ref[h, :, r * rows : (r + 1) * rows] = ref[
                :, width + h * HEAD : width + (h + 1) * HEAD
            ].T
            grad = grad_refs[r][:, lanes]
            up_ref[h, block, :] = grad
            out = mixed_refs[r // 2][(r % 2) * rows : (r % 2 + 1) * rows, lanes]
            both = grad.astype(F32) * out.astype(F32)
            delta_ref[h, :, r * rows : (r + 1) * rows] = jnp.sum(both.T, axis=0, keepdims=True)

    def one_head(h, carry):
        for part in range(2):
            block = pl.ds(part * half, half)
            scores = product_nt(keys_ref[h], query_ref[h, block, :])
            weights = jnp.exp2(scores * (scale * log2e) - log_refs[part][h])
            grad_weights = product_nt(values_ref[h], up_ref[h, block, :])
            grad_scores = (weights * (grad_weights - delta_ref[h, :, block])).astype(BF)
            dq_ref[h, :, block] = product(keys_flat_ref[h], grad_scores) * scale
            dk = product(grad_scores, query_ref[h, block, :])
            dv = product(weights.astype(BF), up_ref[h, block, :])
            if part == 0:
                dk_ref[h] = dk
                dv_ref[h] = dv
            else:
                dk_ref[h] = (dk_ref[h] + dk) * scale
                dv_ref[h] = dv_ref[h] + dv
        return carry

    lax.fori_loop(0, heads, one_head, 0)
    for h in range(heads):
        result_ref[:, h * HEAD : (h + 1) * HEAD] = dq_ref[h].T.astype(BF)
        result_ref[:, width + h * HEAD : width + (h + 1) * HEAD] = dk_ref[h, :, :HEAD].astype(BF)
        result_ref[:, 2 * width + h * HEAD : 2 * width + (h + 1) * HEAD] = dv_ref[h].astype(BF)


def attend_back(quarters, aux_query, aux_key, mixed, logs, grads):
    rows = quarters[0].shape[0]
    length = 4 * rows
    heads = quarters[0].shape[1] // (3 * HEAD)
    whole = pl.BlockSpec(memory_space=pltpu.VMEM)
    return pl.pallas_call(
        functools.partial(backward_body, heads),
        in_specs=[whole] * 14,
        out_specs=whole,
        out_shape=jax.ShapeDtypeStruct((length, 3 * heads * HEAD), BF),
        scratch_shapes=[
            pltpu.VMEM((heads, length, 2 * HEAD), BF),
            pltpu.VMEM((heads, length, 2 * HEAD), BF),
            pltpu.VMEM((heads, length, HEAD), BF),
            pltpu.VMEM((heads, length, HEAD), BF),
            pltpu.VMEM((heads, HEAD, length), BF),
            pltpu.VMEM((heads, 1, length), F32),
            pltpu.VMEM((heads, HEAD, length), F32),
            pltpu.VMEM((heads, length, 2 * HEAD), F32),
            pltpu.VMEM((heads, length, HEAD), F32),
        ],
        compiler_params=pltpu.CompilerParams(vmem_limit_bytes=vmem_bytes),
        cost_estimate=pl.CostEstimate(
            flops=10 * heads * length * length * HEAD * 4,
            bytes_accessed=12 * length * 576,
            transcendentals=heads * length * length,
        ),
        name="attend_back",
    )(*quarters, aux_query, aux_key, *mixed, *logs, *grads)


def exchanger(axis_dp, axis_tensor):
    def swap(values, dp_bits, tensor_bits):
        pairs = [
            (d * axis_tensor + t, (d ^ dp_bits) * axis_tensor + (t ^ tensor_bits))
            for d in range(axis_dp)
            for t in range(axis_tensor)
        ]
        return lax.ppermute(values, ("dp", "tensor"), pairs)

    return swap


def gather_bits(values, bits, swap):
    for bit in bits:
        values = jnp.concatenate([values, swap(values, bit, 0)], axis=0)
    return values


def block_order(device, count, bits):
    order = []
    for block in range(count):
        other = device ^ block
        place = jnp.int32(0)
        for i, bit in enumerate(bits):
            place = place + jnp.where((other & bit) != 0, 1 << i, 0)
        order.append(place)
    return order


def to_natural(values, order):
    rows = values.shape[0] // len(order)
    return jnp.concatenate(
        [lax.dynamic_slice_in_dim(values, place * rows, rows, 0) for place in order], axis=0
    )


def from_natural(values, device, bits):
    count = 1 << len(bits)
    rows = values.shape[0] // count
    blocks = []
    for place in range(count):
        other = sum(bit for i, bit in enumerate(bits) if place >> i & 1)
        blocks.append(lax.dynamic_slice_in_dim(values, (device ^ other) * rows, rows, 0))
    return jnp.concatenate(blocks, axis=0)


def fold_bits(values, bits, swap):
    for bit in reversed(bits):
        half = values.shape[0] // 2
        moved = swap(values[half:].astype(BF), bit, 0)
        values = values[:half].astype(F32) + moved.astype(F32)
    return values


def local(
    axis_dp,
    axis_tensor,
    inputs,
    segments,
    query_weight,
    query_bias,
    key_weight,
    value_weight,
    value_bias,
    output_weight,
    output_bias,
    up_weight,
    up_bias,
    down_weight,
    down_bias,
    first_gain,
    first_shift,
    second_gain,
    second_shift,
    cotangent,
):
    swap = exchanger(axis_dp, axis_tensor)
    device = lax.axis_index("dp")
    levels = axis_dp.bit_length() - 1
    bits = [1 << i for i in reversed(range(levels))]
    order = block_order(device, axis_dp, bits)
    rows, width = inputs.shape[1:]

    own = inputs[0]
    across = swap(own, 0, 2)
    docs = segments[0]
    docs = jnp.concatenate([docs, swap(docs, 0, 1)])
    docs = jnp.concatenate([docs, swap(docs, 0, 2)])
    own_qkv = jnp.concatenate([query_weight, key_weight, value_weight], axis=1)
    qkv_weight = gather_bits(own_qkv, bits, swap)
    tokens = [own, swap(own, 0, 1), across, swap(across, 0, 1)]

    bundle = jnp.concatenate([up_weight, output_weight.T, down_weight.T], axis=1)
    units = up_weight.shape[1]
    feats = output_weight.shape[0]
    bundle = gather_bits(bundle, bits[:-1], swap)
    last = bits[-1]
    bundle_a, bundle_b = bundle[:, : units + feats], bundle[:, units + feats :]
    bundle_a = jnp.concatenate([bundle_a, swap(bundle_a, last, 0)], axis=0)
    bundle_b2 = swap(bundle_b, 0, 2)
    bundle_a2 = swap(bundle_a, 0, 2)
    bundle_b = jnp.concatenate([bundle_b, swap(bundle_b, last, 0)], axis=0)
    bundle_b2 = jnp.concatenate([bundle_b2, swap(bundle_b2, last, 0)], axis=0)
    bundle_a = to_natural(bundle_a, order)
    bundle_a2 = to_natural(bundle_a2, order)
    bundle_b = to_natural(bundle_b, order)
    bundle_b2 = to_natural(bundle_b2, order)
    bundles_a = [bundle_a, swap(bundle_a, 0, 1), bundle_a2, swap(bundle_a2, 0, 1)]
    bundles_b = [bundle_b, swap(bundle_b, 0, 1), bundle_b2, swap(bundle_b2, 0, 1)]
    bias = up_bias.reshape(1, -1)
    bias = jnp.concatenate([bias, swap(bias, 0, 1)])
    bias = jnp.concatenate([bias, swap(bias, 0, 2)])

    qkv_weight = to_natural(qkv_weight, order)
    qkv_bias = jnp.concatenate(
        [query_bias, jnp.zeros_like(query_bias), value_bias]
    ).astype(F32)
    quarters = [(product(x, qkv_weight) + qkv_bias).astype(BF) for x in tokens]

    lane = lax.broadcasted_iota(jnp.int32, (1, HEAD), 1)
    same = docs[:, None] == lane
    aux_query = same.astype(BF)
    aux_key = jnp.where(same | (lane >= 8), 0.0, -far).astype(BF)
    half = 2 * rows
    mixed_other, log_other = attend_forward(quarters, aux_query[half:], aux_key, (2, 3))
    mixed_own, log_own = attend_forward(quarters, aux_query[:half], aux_key, (0, 1))
    mixed = [
        mixed_own[:rows],
        swap(mixed_own[rows:], 0, 1),
        swap(mixed_other[:rows], 0, 2),
        swap(mixed_other[rows:], 0, 3),
    ]

    attn = sum(product_nt(m, b[:, units:]) for m, b in zip(mixed, bundles_a))
    hidden = own.astype(F32) + attn + output_bias
    normed_first, unit_first, inverse_first = normalize(hidden, first_gain, first_shift)
    low = normed_first.astype(BF)
    activated, slopes = [], []
    ffn = 0.0
    for g in range(4):
        inner = product(low, bundles_a[g][:, :units]) + bias[g]
        both = 0.5 * (1.0 + lax.erf(inner * root_half))
        activated.append((inner * both).astype(BF))
        slopes.append((both + inner * density * jnp.exp(-0.5 * inner * inner)).astype(BF))
        ffn = ffn + product_nt(activated[g], bundles_b[g])
    second_in = normed_first + ffn + down_bias
    layer_out, unit_second, inverse_second = normalize(second_in, second_gain, second_shift)
    upstream = cotangent[0].astype(F32)
    grad_second = norm_back(upstream, unit_second, inverse_second, second_gain)
    second_low = grad_second.astype(BF)
    grad_inner = []
    back = 0.0
    for g in range(4):
        grad = product(second_low, bundles_b[g])
        grad_inner.append((grad * slopes[g].astype(F32)).astype(BF))
        back = back + product_nt(grad_inner[g], bundles_a[g][:, :units])
    grad_first = grad_second + back
    grad_hidden = norm_back(grad_first, unit_first, inverse_first, first_gain)
    grad_attn = grad_hidden.astype(BF)
    grad_mixed = [product(grad_attn, b[:, units:]).astype(BF) for b in bundles_a]
    upstreams = [
        grad_mixed[0],
        swap(grad_mixed[1], 0, 1),
        swap(grad_mixed[2], 0, 2),
        swap(grad_mixed[3], 0, 3),
    ]

    grads_a = [
        jnp.concatenate(
            [product_tn(low, grad_inner[g]), product_tn(grad_attn, mixed[g])], axis=1
        ).astype(BF)
        for g in range(4)
    ]
    grads_b = [product_tn(second_low, activated[g]).astype(BF) for g in range(4)]

    def add(left, right):
        return (left.astype(F32) + right.astype(F32)).astype(BF)

    a0 = add(grads_a[0], swap(grads_a[1], 0, 1))
    a2 = add(grads_a[2], swap(grads_a[3], 0, 1))
    b0 = add(grads_b[0], swap(grads_b[1], 0, 1))
    b2 = add(grads_b[2], swap(grads_b[3], 0, 1))
    a0, a2, b0, b2 = (from_natural(v, device, bits) for v in (a0, a2, b0, b2))
    part_a = add(a0, swap(a2, 0, 2))
    own_a = fold_bits(part_a, bits, swap)
    b0 = fold_bits(b0, bits[-1:], swap)
    b2 = fold_bits(b2, bits[-1:], swap).astype(BF)
    part_b = b0 + swap(b2, 0, 2).astype(F32)
    own_b = fold_bits(part_b, bits[:-1], swap)

    column = functools.partial(jnp.sum, axis=0)
    sums = jnp.stack(
        [
            column(grad_hidden),
            column(grad_second),
            column(grad_first * unit_first),
            column(grad_first),
            column(upstream * unit_second),
            column(upstream),
        ]
    )
    sum_up = [column(g.astype(F32)) for g in grad_inner]
    up_pair = jnp.stack([sum_up[0], sum_up[2], sum_up[1], sum_up[3]])
    moved = swap(jnp.concatenate([sums, up_pair[2:]]), 0, 1)
    sums, up_pair = sums + moved[:6], up_pair[:2] + moved[6:]
    moved = swap(jnp.concatenate([sums, up_pair[1:]]), 0, 2)
    totals = jnp.concatenate([sums + moved[:6], up_pair[:1] + moved[6:]])
    for bit in bits:
        totals = totals + swap(totals, bit, 0)

    grad_qkv = attend_back(
        quarters, aux_query, aux_key, (mixed_own, mixed_other), (log_own, log_other), upstreams
    )
    all_tokens = jnp.concatenate(tokens, axis=0)
    back_rows = [
        product_nt(grad_qkv[r * rows : (r + 1) * rows], qkv_weight) for r in range(4)
    ]
    moved = swap(jnp.concatenate([back_rows[1], back_rows[3]]).astype(BF), 0, 1)
    far_rows = (back_rows[2] + moved[rows:].astype(F32)).astype(BF)
    near_rows = back_rows[0] + moved[:rows].astype(F32)
    grad_inputs = grad_hidden + near_rows + swap(far_rows, 0, 2).astype(F32)

    grads_qkv = product_tn(all_tokens, grad_qkv).astype(BF)
    own_qkv = fold_bits(from_natural(grads_qkv, device, bits), bits, swap)
    head_sums = column(grad_qkv.astype(F32)).reshape(1, -1)
    for bit in bits:
        head_sums = head_sums + swap(head_sums, bit, 0)
    head_sums = head_sums[0]

    return (
        layer_out.astype(BF)[None],
        grad_inputs[None],
        own_qkv[:, :feats],
        head_sums[:feats],
        own_qkv[:, feats : 2 * feats],
        own_qkv[:, 2 * feats :],
        head_sums[2 * feats :],
        own_a[:, units:].T,
        totals[0],
        own_a[:, :units],
        totals[6],
        own_b.T,
        totals[1],
        totals[2],
        totals[3],
        totals[4],
        totals[5],
    )


def solution(mesh):
    axis_dp, axis_tensor = mesh.shape["dp"], mesh.shape["tensor"]
    if axis_tensor != 4 or axis_dp & (axis_dp - 1):
        raise ValueError("mesh sizes")
    return jax.shard_map(
        functools.partial(local, axis_dp, axis_tensor),
        mesh=mesh,
        in_specs=(
            P("dp", "tensor", None),
            P("dp", "tensor"),
            P("dp", "tensor"),
            P("tensor"),
            P("dp", "tensor"),
            P("dp", "tensor"),
            P("tensor"),
            P("tensor", "dp"),
            P(),
            P("dp", "tensor"),
            P("tensor"),
            P("tensor", "dp"),
            P(),
            P(),
            P(),
            P(),
            P(),
            P("dp", "tensor", None),
        ),
        out_specs=(
            P("dp", "tensor", None),
            P("dp", "tensor", None),
            P("dp", "tensor"),
            P("tensor"),
            P("dp", "tensor"),
            P("dp", "tensor"),
            P("tensor"),
            P("tensor", "dp"),
            P(),
            P("dp", "tensor"),
            P("tensor"),
            P("tensor", "dp"),
            P(),
            P(),
            P(),
            P(),
            P(),
        ),
        check_vma=False,
    )
```

time: 1210 us -> 419 us (0.35)
  waiting for transfers between devices: 658 us -> 124 us
  blocking collectives: 173 us -> 0 us
  matrix products: 218 us -> 74 us
  Pallas kernels: 0 us -> 71 us
  other arithmetic: 83.3 us -> 45.2 us
  starting transfers between devices: 1.19 us -> 35.7 us
  local copies, waits for them, and re-layouts: 30.5 us -> 59 us
  loops' own time: 18 us -> 0 us
  between operations: 16.3 us -> 2.27 us
    reduce_scatter x6 -> x0, waiting for transfers between devices: 336 us -> none  [the longest x1 73.1 us: local(): lax.psum_scatter(down_weight_gradient, 'dp', scatter_dimension=1, tiled=T...]
    unnamed x20 -> x0, waiting for transfers between devices: 201 us -> none
    dot_general x45, matrix products: 214 us -> 74 us  [the longest x16 27.1 us: product(): return jnp.dot(left, right, preferred_element_type=F32)]
    all_gather x5 -> x0, blocking collectives: 132 us -> none  [the longest x1 31.9 us: local(): lax.all_gather(output_weight, 'dp', axis=1, tiled=True)]
    ppermute x0 -> x53, waiting for transfers between devices: none -> 124 us  [swap(): return lax.ppermute(values, ('dp', 'tensor'), pairs)]
    all_gather x6 -> x0, waiting for transfers between devices: 121 us -> none  [the longest x1 36.6 us: local(): lax.all_gather(down_weight, 'dp', axis=1, tiled=True)]
    pallas_call x0 -> x3, Pallas kernels: none -> 71 us  [the longest x1 41.9 us: attend_back(): pl.pallas_call(functools.partial(backward_body, heads), in_specs=[whole]...]
    psum x1 -> x0, blocking collectives: 40.8 us -> none  [local(): lax.psum((place_query, place_value, place_up, sum_output, sum_down, gain_...]
  transfers between devices with their start and end apart: 16 -> 53, of which waited for: 13 -> 23; matrix products, arithmetic and copies ran while one was open for 5% -> 34% of each run, Pallas kernels for 0% -> 17%
where the time goes in v1:
time: 419 us; the launch traced here: 411 us
  waiting for transfers between devices  124 us (30%)
  matrix products  74 us (18%)
  Pallas kernels  71 us (17%)
  local copies, waits for them, and re-layouts  59 us (14%)
  other arithmetic  45.2 us (11%)
  starting transfers between devices  35.7 us (9%)
    ppermute x53, waiting for transfers between devices, swap(): return lax.ppermute(values, ('dp', 'tensor'), pairs)  124 us
    pallas_call x1, Pallas kernels, attend_back(): pl.pallas_call(functools.partial(backward_body, heads), in_specs=[whole]...  41.9 us
    ppermute x53, starting transfers between devices, swap(): return lax.ppermute(values, ('dp', 'tensor'), pairs)  35.7 us
    pallas_call x2, Pallas kernels, attend_forward(): pl.pallas_call(functools.partial(forward_body, heads), in_specs=[whole] *...  29 us
    dot_general x16, matrix products, product(): return jnp.dot(left, right, preferred_element_type=F32)  27.1 us
    dot_general x13, matrix products, product_tn(): lax.dot_general(left, right, (((0,), (0,)), ((), ())), preferred_element_...  24.6 us
    dot_general x16, matrix products, product_nt(): lax.dot_general(left, right, (((1,), (1,)), ((), ())), preferred_element_...  22.2 us
    unnamed x120, local copies, waits for them, and re-layouts  12.1 us
  transfers between devices with their start and end apart: 53, of which 23 were waited for; matrix products, arithmetic and copies ran while one was open for 34% of the time, Pallas kernels for 17%

profile of v1, /device:TPU:0, one launch (start us, length us, event | category | flops | bytes accessed | tf_op | source)
XLA Modules:
  0.0 411.0 jit_solution(7094818047902217730)
XLA Ops:
  1.3 2.6 collective-permute-start.4
  5.6 2.7 collective-permute-start
  15.9 6.5 %collective-permute-done.20 = bf16[2,768]{1,0:T(2,128)(2,1)S(1)} collective-permute-done((bf16[2,768]{1,0:T(2,128)(2,1)S(1)}, bf16[2,768]{1,0:T(2,128)(2,1)S(1)}, u32[]{:S(2)}, u32[]{:S(2)}) %collective-permute-start.20) | collective-permute-done | bytes 3104 | tf_op jit(solution)/shard_map/ppermute | solution.py:212
  22.3 1.7 collective-permute-start.7
  27.3 1.9 collective-permute-start.1
  29.5 8.7 %collective-permute-done.1 = bf16[192,576]{1,0:T(8,128)(2,1)S(1)} collective-permute-done((bf16[192,576]{1,0:T(8,128)(2,1)S(1)}, bf16[192,576]{1,0:T(8,128)(2,1)S(1)}, u32[]{:S(2)}, u32[]{:S(2)}) %collective-permute-start.1) | collective-permute-done | bytes 221216 | tf_op jit(solution)/shard_map/ppermute | solution.py:212
  40.8 10.7 %collective-permute-done.2 = bf16[384,576]{1,0:T(8,128)(2,1)S(1)} collective-permute-done((bf16[384,576]{1,0:T(8,128)(2,1)S(1)}, bf16[384,576]{1,0:T(8,128)(2,1)S(1)}, u32[]{:S(2)}, u32[]{:S(2)}) %collective-permute-start.2) | collective-permute-done | bytes 442400 | tf_op jit(solution)/shard_map/ppermute | solution.py:212
  53.6 2.8 fusion.42.refs_2_.refs_6_
  56.4 2.8 fusion.43.refs_1_.refs_7_
  63.4 2.8 fusion.41.refs_3_.refs_7_
  66.2 14.6 %attend_forward.3 = (bf16[1024,192]{1,0:T(8,128)(2,1)}, f32[3,1,1024]{2,1,0:T(1,128)}) custom-call(bf16[512,576]{1,0:T(8,128)(2,1)} %fusion.44.refs_0_.refs_6_, bf16[512,576]{1,0:T(8,128)(2,1)} %fusion.43.refs_1_.refs_7_, bf16[512,576]{1,0:T(8,128)(2,1)} %fusion.42.refs_2_.refs_6_, bf16[512,576]{1,0:T(8,128)(2,1)} %fusion.41.refs_3_.refs_7_, ...), custom_call_target="tpu_custom_call" | custom-call | flops 6442450944 | bytes 9437184 | tf_op jit(solution)/shard_map/attend_forward/pallas_call | solution.py:103
  80.8 1.9 fusion.123
  84.2 14.4 %attend_forward.2 = (bf16[1024,192]{1,0:T(8,128)(2,1)}, f32[3,1,1024]{2,1,0:T(1,128)}) custom-call(bf16[512,576]{1,0:T(8,128)(2,1)} %fusion.44.refs_0_.refs_6_, bf16[512,576]{1,0:T(8,128)(2,1)} %fusion.43.refs_1_.refs_7_, bf16[512,576]{1,0:T(8,128)(2,1)} %fusion.42.refs_2_.refs_6_, bf16[512,576]{1,0:T(8,128)(2,1)} %fusion.41.refs_3_.refs_7_, ...), custom_call_target="tpu_custom_call" | custom-call | flops 6442450944 | bytes 9437184 | tf_op jit(solution)/shard_map/attend_forward/pallas_call | solution.py:103
  106.6 2.6 copy.91
  111.5 1.9 constant_dynamic-update-slice_fusion.1
  119.6 2.7 copy.90
  125.0 18.6 %collective-permute-done.14 = bf16[768,960]{0,1:T(8,128)(2,1)} collective-permute-done((bf16[768,960]{0,1:T(8,128)(2,1)}, bf16[768,960]{0,1:T(8,128)(2,1)}, u32[]{:S(2)}, u32[]{:S(2)}) %collective-permute-start.14) | collective-permute-done | bytes 1474592 | tf_op jit(solution)/shard_map/ppermute | solution.py:212
  143.7 3.9 constant_dynamic-slice_fusion.40
  147.5 4.3 %concatenate.141 = bf16[768,960]{0,1:T(8,128)(2,1)} concatenate(bf16[96,960]{0,1:T(8,128)(2,1)} %get-tuple-element.137, bf16[96,960]{0,1:T(8,128)(2,1)} %get-tuple-element.136, bf16[96,960]{0,1:T(8,128)(2,1)} %get-tuple-element.135, bf16[96,960]{0,1:T(8,128)(2,1)} %get-tuple-element.134, bf16[96,960]{0,1:T(8,128)(2,1)} %get-tuple-element.133, ...), dimensions={0} | concatenate | bytes 2949120 | tf_op jit(solution)/shard_map/concatenate | solution.py:236
  157.9 2.2 multiply_convert_fusion.7
  164.1 2.8 multiply_convert_fusion.6
  176.0 2.1 fusion.58
  180.3 2.1 fusion.55
  187.0 1.8 convolution_convert_fusion.4
  188.9 1.9 convolution_convert_fusion.5
  190.7 1.9 convolution_convert_fusion.6
  193.0 1.8 convolution_convert_fusion.7
  194.8 1.8 convolution_convert_fusion
  196.6 1.9 convolution_convert_fusion.2
  198.5 2.1 convolution_convert_fusion.17
  200.6 1.8 copy.92
  210.6 2.6 pad_maximum_fusion.3
  213.2 5.1 %collective-permute-done.42 = f32[7,768]{1,0:T(8,128)S(1)} collective-permute-done((f32[7,768]{1,0:T(8,128)S(1)}, f32[7,768]{1,0:T(8,128)S(1)}, u32[]{:S(2)}, u32[]{:S(2)}) %collective-permute-start.42) | collective-permute-done | bytes 21536 | tf_op jit(solution)/shard_map/ppermute | solution.py:212
  218.4 2.4 convolution_convert_fusion.11
  220.9 2.3 collective-permute-done.43
  224.6 2.5 collective-permute-done.44
  232.1 41.9 %attend_back.1 = bf16[2048,576]{1,0:T(8,128)(2,1)} custom-call(bf16[512,576]{1,0:T(8,128)(2,1)} %fusion.44.refs_0_.refs_6_, bf16[512,576]{1,0:T(8,128)(2,1)} %fusion.43.refs_1_.refs_7_, bf16[512,576]{1,0:T(8,128)(2,1)} %fusion.42.refs_2_.refs_6_, bf16[512,576]{1,0:T(8,128)(2,1)} %fusion.41.refs_3_.refs_7_, bf16[2048,64]{1,0:T(8,128)(2,1)} %copy-done.7, ...), custom_call_target="tpu_custom_call" | custom-call | flops 32212254720 | bytes 14155776 | tf_op jit(solution)/shard_map/attend_back/pallas_call | solution.py:179
  274.0 2.4 fusion.65
  277.5 3.7 fusion.33
  284.1 3.0 collective-permute-done.32
  287.2 7.1 %collective-permute-done.29 = bf16[384,576]{0,1:T(8,128)(2,1)S(1)} collective-permute-done((bf16[384,576]{0,1:T(8,128)(2,1)S(1)}, bf16[384,576]{0,1:T(8,128)(2,1)S(1)}, u32[]{:S(2)}, u32[]{:S(2)}) %collective-permute-start.29) | collective-permute-done | bytes 442400 | tf_op jit(solution)/shard_map/ppermute | solution.py:212
  297.5 1.8 collective-permute-done.34
  299.3 3.5 collective-permute-done.30
  304.3 7.0 %collective-permute-done.31 = bf16[96,576]{0,1:T(8,128)(2,1)S(1)} collective-permute-done((bf16[96,576]{0,1:T(8,128)(2,1)S(1)}, bf16[96,576]{0,1:T(8,128)(2,1)S(1)}, u32[]{:S(2)}, u32[]{:S(2)}) %collective-permute-start.31) | collective-permute-done | bytes 110624 | tf_op jit(solution)/shard_map/ppermute | solution.py:212
  312.0 3.3 add_convert_fusion.3
  315.3 1.8 add_convert_fusion.1
  317.1 2.0 constant_dynamic-slice_fusion.16
  319.1 4.2 %concatenate.156 = bf16[768,960]{0,1:T(8,128)(2,1)} concatenate(bf16[96,960]{0,1:T(8,128)(2,1)} %get-tuple-element.129, bf16[96,960]{0,1:T(8,128)(2,1)} %get-tuple-element.128, bf16[96,960]{0,1:T(8,128)(2,1)} %get-tuple-element.127, bf16[96,960]{0,1:T(8,128)(2,1)} %get-tuple-element.126, bf16[96,960]{0,1:T(8,128)(2,1)} %get-tuple-element.125, ...), dimensions={0} | concatenate | bytes 2949120 | tf_op jit(solution)/shard_map/concatenate | solution.py:248
  324.8 2.2 constant_dynamic-slice_fusion.7
  328.4 2.1 add_convert_fusion.4
  333.7 1.8 add_convert_fusion.2
  335.5 1.9 constant_dynamic-slice_fusion.24
  337.5 4.0 concatenate.153
  341.5 2.9 collective-permute-done.49
  344.4 2.1 add_convert_fusion.7
  347.1 11.7 %collective-permute-done.37 = bf16[768,960]{0,1:T(8,128)(2,1)} collective-permute-done((bf16[768,960]{0,1:T(8,128)(2,1)}, bf16[768,960]{0,1:T(8,128)(2,1)}, u32[]{:S(2)}, u32[]{:S(2)}) %collective-permute-start.37) | collective-permute-done | bytes 1474592 | tf_op jit(solution)/shard_map/ppermute | solution.py:212
  358.9 1.8 add_convert_fusion
  362.3 3.0 add_convert_fusion.5
  373.3 6.4 %collective-permute-done.38 = bf16[384,960]{0,1:T(8,128)(2,1)} collective-permute-done((bf16[384,960]{0,1:T(8,128)(2,1)}, bf16[384,960]{0,1:T(8,128)(2,1)}, u32[]{:S(2)}, u32[]{:S(2)}) %collective-permute-start.38) | collective-permute-done | bytes 737312 | tf_op jit(solution)/shard_map/ppermute | solution.py:212
  381.2 6.7 %collective-permute-done.28 = bf16[512,768]{1,0:T(8,128)(2,1)} collective-permute-done((bf16[512,768]{1,0:T(8,128)(2,1)}, bf16[512,768]{1,0:T(8,128)(2,1)}, u32[]{:S(2)}, u32[]{:S(2)}) %collective-permute-start.28) | collective-permute-done | bytes 786464 | tf_op jit(solution)/shard_map/ppermute | solution.py:212
  387.9 2.8 add_bitcast_fusion
  390.9 1.8 collective-permute-done.39
  394.1 9.9 %collective-permute-done.52 = bf16[96,768]{1,0:T(8,128)(2,1)S(1)} collective-permute-done((bf16[96,768]{1,0:T(8,128)(2,1)S(1)}, bf16[96,768]{1,0:T(8,128)(2,1)S(1)}, u32[]{:S(2)}, u32[]{:S(2)}) %collective-permute-start.52) | collective-permute-done | bytes 147488 | tf_op jit(solution)/shard_map/ppermute | solution.py:212
  404.8 4.4 %collective-permute-done.40 = bf16[96,960]{0,1:T(8,128)(2,1)S(1)} collective-permute-done((bf16[96,960]{0,1:T(8,128)(2,1)S(1)}, bf16[96,960]{0,1:T(8,128)(2,1)S(1)}, u32[]{:S(2)}, u32[]{:S(2)}) %collective-permute-start.40) | collective-permute-done | bytes 184352 | tf_op jit(solution)/shard_map/ppermute | solution.py:212
  (348 shorter events, 114.4 us)
Async XLA Ops:
  0.7 26.5 %copy-start.29 = (bf16[96,192]{1,0:T(8,128)(2,1)S(1)}, bf16[96,192]{1,0:T(8,128)(2,1)}, u32[]{:S(2)}) copy-start(bf16[96,192]{1,0:T(8,128)(2,1)} %param.23) | copy-start | bytes 110596
  0.7 26.5 %copy-start.30 = (bf16[96,192]{1,0:T(8,128)(2,1)S(1)}, bf16[96,192]{1,0:T(8,128)(2,1)}, u32[]{:S(2)}) copy-start(bf16[96,192]{1,0:T(8,128)(2,1)} %param.22) | copy-start | bytes 110596
  0.7 26.5 %copy-start.31 = (bf16[96,192]{1,0:T(8,128)(2,1)S(1)}, bf16[96,192]{1,0:T(8,128)(2,1)}, u32[]{:S(2)}) copy-start(bf16[96,192]{1,0:T(8,128)(2,1)} %param.20) | copy-start | bytes 110596
  0.7 15.2 %copy-start.43 = (s32[1,512]{1,0:T(1,128)S(1)}, s32[1,512]{1,0:T(1,128)}, u32[]{:S(2)}) copy-start(s32[1,512]{1,0:T(1,128)} %param.19) | copy-start | bytes 6148
  0.7 55.7 %collective-permute-start.3 = (bf16[512,768]{1,0:T(8,128)(2,1)}, bf16[512,768]{1,0:T(8,128)(2,1)}, u32[]{:S(2)}, u32[]{:S(2)}) collective-permute-start(bf16[512,768]{1,0:T(8,128)(2,1)} %bitcast.110), channel_id=1, source_target_pairs={{0,1},{1,0},{2,3},{3,2},{4,5},{5,4},{6,7},{7,6},{8,9},{9,8},{10,11... | collective-permute-start | bytes 2359304 | tf_op jit(solution)/shard_map/ppermute | solution.py:212
  1.3 52.3 %collective-permute-start.4 = (bf16[512,768]{1,0:T(8,128)(2,1)}, bf16[512,768]{1,0:T(8,128)(2,1)}, u32[]{:S(2)}, u32[]{:S(2)}) collective-permute-start(bf16[512,768]{1,0:T(8,128)(2,1)} %bitcast.111), channel_id=1, source_target_pairs={{0,2},{1,3},{2,0},{3,1},{4,6},{5,7},{6,4},{7,5},{8,10},{9,11},{10,... | collective-permute-start | bytes 2359304 | tf_op jit(solution)/shard_map/ppermute | solution.py:212
  4.6 9.7 %collective-permute-start.18 = (bf16[1,768]{1,0:T(2,128)(2,1)S(1)}, bf16[1,768]{1,0:T(2,128)(2,1)S(1)}, u32[]{:S(2)}, u32[]{:S(2)}) collective-permute-start(bf16[1,768]{1,0:T(2,128)(2,1)S(1)} %reshape.115), channel_id=1, source_target_pairs={{0,1},{1,0},{2,3},{3,2},{4,5},{5,4},{6,7},{7,6},{8,9},{9,8},{10,11... | collective-permute-start | bytes 4616 | tf_op jit(solution)/shard_map/ppermute | solution.py:212
  5.6 21.5 %collective-permute-start = (bf16[96,576]{1,0:T(8,128)(2,1)S(1)}, bf16[96,576]{1,0:T(8,128)(2,1)S(1)}, u32[]{:S(2)}, u32[]{:S(2)}) collective-permute-start(bf16[96,576]{1,0:T(8,128)(2,1)S(1)} %pad_maximum_fusion.13), channel_id=1, source_target_pairs={{0,16},{1,17},{2,18},{3,19},{4,20},{5,21},{6,22},{7,23},{8,24},{9,... | collective-permute-start | bytes 331784 | tf_op jit(solution)/shard_map/ppermute | solution.py:212
  8.3 7.0 %collective-permute-start.6 = (s32[512]{0:T(512)}, s32[512]{0:T(512)S(1)}, u32[]{:S(2)}, u32[]{:S(2)}) collective-permute-start(s32[512]{0:T(512)} %bitcast.115), channel_id=1, source_target_pairs={{0,1},{1,0},{2,3},{3,2},{4,5},{5,4},{6,7},{7,6},{8,9},{9,8},{10,11... | collective-permute-start | bytes 6152 | tf_op jit(solution)/shard_map/ppermute | solution.py:212
  14.2 26.5 %collective-permute-start.8 = (bf16[96,1728]{1,0:T(8,128)(2,1)S(1)}, bf16[96,1728]{1,0:T(8,128)(2,1)S(1)}, u32[]{:S(2)}, u32[]{:S(2)}) collective-permute-start(bf16[96,1728]{1,0:T(8,128)(2,1)S(1)} %concatenate.136), channel_id=1, source_target_pairs={{0,16},{1,17},{2,18},{3,19},{4,20},{5,21},{6,22},{7,23},{8,24},{9,... | collective-permute-start | bytes 995336 | tf_op jit(solution)/shard_map/ppermute | solution.py:212
  15.3 7.1 %collective-permute-start.20 = (bf16[2,768]{1,0:T(2,128)(2,1)S(1)}, bf16[2,768]{1,0:T(2,128)(2,1)S(1)}, u32[]{:S(2)}, u32[]{:S(2)}) collective-permute-start(bf16[2,768]{1,0:T(2,128)(2,1)S(1)} %pad_maximum_fusion.16), channel_id=1, source_target_pairs={{0,2},{1,3},{2,0},{3,1},{4,6},{5,7},{6,4},{7,5},{8,10},{9,11},{10,... | collective-permute-start | bytes 9224 | tf_op jit(solution)/shard_map/ppermute | solution.py:212
  22.3 3.6 collective-permute-start.7
  27.3 11.0 %collective-permute-start.1 = (bf16[192,576]{1,0:T(8,128)(2,1)S(1)}, bf16[192,576]{1,0:T(8,128)(2,1)S(1)}, u32[]{:S(2)}, u32[]{:S(2)}) collective-permute-start(bf16[192,576]{1,0:T(8,128)(2,1)S(1)} %pad_maximum_fusion.12), channel_id=1, source_target_pairs={{0,8},{1,9},{2,10},{3,11},{4,12},{5,13},{6,14},{7,15},{8,0},{9,1},... | collective-permute-start | bytes 663560 | tf_op jit(solution)/shard_map/ppermute | solution.py:212
  38.3 13.2 %collective-permute-start.2 = (bf16[384,576]{1,0:T(8,128)(2,1)S(1)}, bf16[384,576]{1,0:T(8,128)(2,1)S(1)}, u32[]{:S(2)}, u32[]{:S(2)}) collective-permute-start(bf16[384,576]{1,0:T(8,128)(2,1)S(1)} %pad_maximum_fusion.10), channel_id=1, source_target_pairs={{0,4},{1,5},{2,6},{3,7},{4,0},{5,1},{6,2},{7,3},{8,12},{9,13},{10,... | collective-permute-start | bytes 1327112 | tf_op jit(solution)/shard_map/ppermute | solution.py:212
  40.8 18.4 %collective-permute-start.9 = (bf16[192,1728]{1,0:T(8,128)(2,1)S(1)}, bf16[192,1728]{1,0:T(8,128)(2,1)S(1)}, u32[]{:S(2)}, u32[]{:S(2)}) collective-permute-start(bf16[192,1728]{1,0:T(8,128)(2,1)S(1)} %pad_maximum_fusion.6), channel_id=1, source_target_pairs={{0,8},{1,9},{2,10},{3,11},{4,12},{5,13},{6,14},{7,15},{8,0},{9,1},... | collective-permute-start | bytes 1990664 | tf_op jit(solution)/shard_map/ppermute | solution.py:212
  53.6 9.8 %collective-permute-start.5 = (bf16[512,768]{1,0:T(8,128)(2,1)}, bf16[512,768]{1,0:T(8,128)(2,1)}, u32[]{:S(2)}, u32[]{:S(2)}) collective-permute-start(bf16[512,768]{1,0:T(8,128)(2,1)} %collective-permute-done.4), channel_id=1, source_target_pairs={{0,1},{1,0},{2,3},{3,2},{4,5},{5,4},{6,7},{7,6},{8,9},{9,8},{10,11... | collective-permute-start | bytes 2359304 | tf_op jit(solution)/shard_map/ppermute | solution.py:212
  59.4 40.9 %collective-permute-start.21 = (bf16[384,768]{1,0:T(8,128)(2,1)S(1)}, bf16[384,768]{1,0:T(8,128)(2,1)}, u32[]{:S(2)}, u32[]{:S(2)}) collective-permute-start(bf16[384,768]{1,0:T(8,128)(2,1)S(1)} %pad_maximum_fusion.7), channel_id=1, source_target_pairs={{0,2},{1,3},{2,0},{3,1},{4,6},{5,7},{6,4},{7,5},{8,10},{9,11},{10,... | collective-permute-start | bytes 1769480 | tf_op jit(solution)/shard_map/ppermute | solution.py:212
  60.0 40.6 %collective-permute-start.17 = (bf16[384,768]{1,0:T(8,128)(2,1)S(1)}, bf16[384,768]{1,0:T(8,128)(2,1)S(1)}, u32[]{:S(2)}, u32[]{:S(2)}) collective-permute-start(bf16[384,768]{1,0:T(8,128)(2,1)S(1)} %pad_maximum_fusion.7), channel_id=1, source_target_pairs={{0,4},{1,5},{2,6},{3,7},{4,0},{5,1},{6,2},{7,3},{8,12},{9,13},{10,... | collective-permute-start | bytes 1769480 | tf_op jit(solution)/shard_map/ppermute | solution.py:212
  62.8 41.0 %collective-permute-start.10 = (bf16[384,960]{0,1:T(8,128)(2,1)}, bf16[384,960]{0,1:T(8,128)(2,1)}, u32[]{:S(2)}, u32[]{:S(2)}) collective-permute-start(bf16[384,960]{0,1:T(8,128)(2,1)} %copy.88), channel_id=1, source_target_pairs={{0,4},{1,5},{2,6},{3,7},{4,0},{5,1},{6,2},{7,3},{8,12},{9,13},{10,... | collective-permute-start | bytes 2211848 | tf_op jit(solution)/shard_map/ppermute | solution.py:212
  82.7 73.4 %collective-permute-start.15 = (bf16[512,192]{1,0:T(8,128)(2,1)}, bf16[512,192]{1,0:T(8,128)(2,1)S(1)}, u32[]{:S(2)}, u32[]{:S(2)}) collective-permute-start(bf16[512,192]{1,0:T(8,128)(2,1)} %get-tuple-element.162), channel_id=1, source_target_pairs={{0,3},{1,2},{2,1},{3,0},{4,7},{5,6},{6,5},{7,4},{8,11},{9,10},{10,... | collective-permute-start | bytes 589832 | tf_op jit(solution)/shard_map/ppermute | solution.py:212
  83.5 68.7 %collective-permute-start.13 = (bf16[512,192]{1,0:T(8,128)(2,1)}, bf16[512,192]{1,0:T(8,128)(2,1)}, u32[]{:S(2)}, u32[]{:S(2)}) collective-permute-start(bf16[512,192]{1,0:T(8,128)(2,1)} %get-tuple-element.163), channel_id=1, source_target_pairs={{0,2},{1,3},{2,0},{3,1},{4,6},{5,7},{6,4},{7,5},{8,10},{9,11},{10,... | collective-permute-start | bytes 589832 | tf_op jit(solution)/shard_map/ppermute | solution.py:212
  100.3 54.3 %collective-permute-start.11 = (bf16[512,192]{1,0:T(8,128)(2,1)}, bf16[512,192]{1,0:T(8,128)(2,1)}, u32[]{:S(2)}, u32[]{:S(2)}) collective-permute-start(bf16[512,192]{1,0:T(8,128)(2,1)} %slice.214), channel_id=1, source_target_pairs={{0,1},{1,0},{2,3},{3,2},{4,5},{5,4},{6,7},{7,6},{8,9},{9,8},{10,11... | collective-permute-start | bytes 589832 | tf_op jit(solution)/shard_map/ppermute | solution.py:212
  100.6 23.2 %collective-permute-start.22 = (bf16[384,768]{1,0:T(8,128)(2,1)}, bf16[384,768]{1,0:T(8,128)(2,1)}, u32[]{:S(2)}, u32[]{:S(2)}) collective-permute-start(bf16[384,768]{1,0:T(8,128)(2,1)} %collective-permute-done.21), channel_id=1, source_target_pairs={{0,4},{1,5},{2,6},{3,7},{4,0},{5,1},{6,2},{7,3},{8,12},{9,13},{10,... | collective-permute-start | bytes 1769480 | tf_op jit(solution)/shard_map/ppermute | solution.py:212
  109.2 34.4 %collective-permute-start.14 = (bf16[768,960]{0,1:T(8,128)(2,1)}, bf16[768,960]{0,1:T(8,128)(2,1)}, u32[]{:S(2)}, u32[]{:S(2)}) collective-permute-start(bf16[768,960]{0,1:T(8,128)(2,1)} %copy.91), channel_id=1, source_target_pairs={{0,2},{1,3},{2,0},{3,1},{4,6},{5,7},{6,4},{7,5},{8,10},{9,11},{10,... | collective-permute-start | bytes 4423688 | tf_op jit(solution)/shard_map/ppermute | solution.py:212
  123.8 30.8 %collective-permute-start.12 = (bf16[768,960]{0,1:T(8,128)(2,1)}, bf16[768,960]{0,1:T(8,128)(2,1)}, u32[]{:S(2)}, u32[]{:S(2)}) collective-permute-start(bf16[768,960]{0,1:T(8,128)(2,1)} %copy.90), channel_id=1, source_target_pairs={{0,1},{1,0},{2,3},{3,2},{4,5},{5,4},{6,7},{7,6},{8,9},{9,8},{10,11... | collective-permute-start | bytes 4423688 | tf_op jit(solution)/shard_map/ppermute | solution.py:212
  151.8 4.3 %collective-permute-start.16 = (bf16[768,960]{0,1:T(8,128)(2,1)}, bf16[768,960]{0,1:T(8,128)(2,1)S(1)}, u32[]{:S(2)}, u32[]{:S(2)}) collective-permute-start(bf16[768,960]{0,1:T(8,128)(2,1)} %concatenate.141), channel_id=1, source_target_pairs={{0,1},{1,0},{2,3},{3,2},{4,5},{5,4},{6,7},{7,6},{8,9},{9,8},{10,11... | collective-permute-start | bytes 4423688 | tf_op jit(solution)/shard_map/ppermute | solution.py:212
  152.2 14.8 %collective-permute-start.19 = (bf16[768,768]{1,0:T(8,128)(2,1)}, bf16[768,768]{1,0:T(8,128)(2,1)S(1)}, u32[]{:S(2)}, u32[]{:S(2)}) collective-permute-start(bf16[768,768]{1,0:T(8,128)(2,1)} %fusion.108), channel_id=1, source_target_pairs={{0,1},{1,0},{2,3},{3,2},{4,5},{5,4},{6,7},{7,6},{8,9},{9,8},{10,11... | collective-permute-start | bytes 3538952 | tf_op jit(solution)/shard_map/ppermute | solution.py:212
  154.5 7.9 %collective-permute-start.23 = (bf16[768,768]{1,0:T(8,128)(2,1)S(1)}, bf16[768,768]{1,0:T(8,128)(2,1)S(1)}, u32[]{:S(2)}, u32[]{:S(2)}) collective-permute-start(bf16[768,768]{1,0:T(8,128)(2,1)S(1)} %dynamic-slice_dynamic-update-slice_fusion), channel_id=1, source_target_pairs={{0,1},{1,0},{2,3},{3,2},{4,5},{5,4},{6,7},{7,6},{8,9},{9,8},{10,11... | collective-permute-start | bytes 3538952 | tf_op jit(solution)/shard_map/ppermute | solution.py:212
  156.1 26.3 %copy-start.10 = (bf16[768,960]{0,1:T(8,128)(2,1)}, bf16[768,960]{0,1:T(8,128)(2,1)S(1)}, u32[]{:S(2)}) copy-start(bf16[768,960]{0,1:T(8,128)(2,1)S(1)} %collective-permute-done.16) | copy-start | bytes 4423684
  172.9 23.8 %copy-start.26 = (bf16[512,768]{1,0:T(8,128)(2,1)}, bf16[512,768]{1,0:T(8,128)(2,1)S(1)}, u32[]{:S(2)}) copy-start(bf16[512,768]{1,0:T(8,128)(2,1)S(1)} %convert_element_type.298) | copy-start | bytes 2359300
  202.4 29.2 %collective-permute-start.24 = (bf16[512,192]{1,0:T(8,128)(2,1)}, bf16[512,192]{1,0:T(8,128)(2,1)}, u32[]{:S(2)}, u32[]{:S(2)}) collective-permute-start(bf16[512,192]{1,0:T(8,128)(2,1)} %copy.92), channel_id=1, source_target_pairs={{0,1},{1,0},{2,3},{3,2},{4,5},{5,4},{6,7},{7,6},{8,9},{9,8},{10,11... | collective-permute-start | bytes 589832 | tf_op jit(solution)/shard_map/ppermute | solution.py:212
  203.7 28.4 %collective-permute-start.25 = (bf16[512,192]{1,0:T(8,128)(2,1)}, bf16[512,192]{1,0:T(8,128)(2,1)}, u32[]{:S(2)}, u32[]{:S(2)}) collective-permute-start(bf16[512,192]{1,0:T(8,128)(2,1)} %copy.93), channel_id=1, source_target_pairs={{0,2},{1,3},{2,0},{3,1},{4,6},{5,7},{6,4},{7,5},{8,10},{9,11},{10,... | collective-permute-start | bytes 589832 | tf_op jit(solution)/shard_map/ppermute | solution.py:212
  207.3 24.8 %collective-permute-start.26 = (bf16[512,192]{1,0:T(8,128)(2,1)}, bf16[512,192]{1,0:T(8,128)(2,1)}, u32[]{:S(2)}, u32[]{:S(2)}) collective-permute-start(bf16[512,192]{1,0:T(8,128)(2,1)} %copy.94), channel_id=1, source_target_pairs={{0,3},{1,2},{2,1},{3,0},{4,7},{5,6},{6,5},{7,4},{8,11},{9,10},{10,... | collective-permute-start | bytes 589832 | tf_op jit(solution)/shard_map/ppermute | solution.py:212
  207.4 1.6 collective-permute-start.41
  209.1 9.2 %collective-permute-start.42 = (f32[7,768]{1,0:T(8,128)S(1)}, f32[7,768]{1,0:T(8,128)S(1)}, u32[]{:S(2)}, u32[]{:S(2)}) collective-permute-start(f32[7,768]{1,0:T(8,128)S(1)} %pad_maximum_fusion.14), channel_id=1, source_target_pairs={{0,2},{1,3},{2,0},{3,1},{4,6},{5,7},{6,4},{7,5},{8,10},{9,11},{10,... | collective-permute-start | bytes 64520 | tf_op jit(solution)/shard_map/ppermute | solution.py:212
  213.2 14.4 %copy-start.20 = (bf16[768,768]{0,1:T(8,128)(2,1)S(1)}, bf16[768,768]{0,1:T(8,128)(2,1)}, u32[]{:S(2)}) copy-start(bf16[768,768]{0,1:T(8,128)(2,1)} %convolution_convert_fusion.6) | copy-start | bytes 3538948
  213.2 102.1 %collective-permute-start.36 = (bf16[768,960]{0,1:T(8,128)(2,1)}, bf16[768,960]{0,1:T(8,128)(2,1)}, u32[]{:S(2)}, u32[]{:S(2)}) collective-permute-start(bf16[768,960]{0,1:T(8,128)(2,1)} %pad_maximum_fusion.3), channel_id=1, source_target_pairs={{0,1},{1,0},{2,3},{3,2},{4,5},{5,4},{6,7},{7,6},{8,9},{9,8},{10,11... | collective-permute-start | bytes 4423688 | tf_op jit(solution)/shard_map/ppermute | solution.py:212
  218.4 4.8 %collective-permute-start.43 = (f32[7,768]{1,0:T(8,128)S(1)}, f32[7,768]{1,0:T(8,128)S(1)}, u32[]{:S(2)}, u32[]{:S(2)}) collective-permute-start(f32[7,768]{1,0:T(8,128)S(1)} %pad_maximum_fusion.15), channel_id=1, source_target_pairs={{0,16},{1,17},{2,18},{3,19},{4,20},{5,21},{6,22},{7,23},{8,24},{9,... | collective-permute-start | bytes 64520 | tf_op jit(solution)/shard_map/ppermute | solution.py:212
  223.2 3.9 collective-permute-start.44
  227.1 3.8 collective-permute-start.45
  230.9 102.9 %collective-permute-start.35 = (bf16[768,960]{0,1:T(8,128)(2,1)}, bf16[768,960]{0,1:T(8,128)(2,1)}, u32[]{:S(2)}, u32[]{:S(2)}) collective-permute-start(bf16[768,960]{0,1:T(8,128)(2,1)} %pad_maximum_fusion.2), channel_id=1, source_target_pairs={{0,1},{1,0},{2,3},{3,2},{4,5},{5,4},{6,7},{7,6},{8,9},{9,8},{10,11... | collective-permute-start | bytes 4423688 | tf_op jit(solution)/shard_map/ppermute | solution.py:212
  231.6 80.4 %collective-permute-start.48 = (bf16[768,768]{1,0:T(8,128)(2,1)}, bf16[768,768]{1,0:T(8,128)(2,1)}, u32[]{:S(2)}, u32[]{:S(2)}) collective-permute-start(bf16[768,768]{1,0:T(8,128)(2,1)} %convolution_convert_fusion), channel_id=1, source_target_pairs={{0,1},{1,0},{2,3},{3,2},{4,5},{5,4},{6,7},{7,6},{8,9},{9,8},{10,11... | collective-permute-start | bytes 3538952 | tf_op jit(solution)/shard_map/ppermute | solution.py:212
  282.1 12.2 %collective-permute-start.29 = (bf16[384,576]{0,1:T(8,128)(2,1)S(1)}, bf16[384,576]{0,1:T(8,128)(2,1)S(1)}, u32[]{:S(2)}, u32[]{:S(2)}) collective-permute-start(bf16[384,576]{0,1:T(8,128)(2,1)S(1)} %pad_maximum_fusion.11), channel_id=1, source_target_pairs={{0,4},{1,5},{2,6},{3,7},{4,0},{5,1},{6,2},{7,3},{8,12},{9,13},{10,... | collective-permute-start | bytes 1327112 | tf_op jit(solution)/shard_map/ppermute | solution.py:212
  282.7 4.5 %collective-permute-start.32 = (f32[1,576]{1,0:T(1,128)S(1)}, f32[1,576]{1,0:T(1,128)S(1)}, u32[]{:S(2)}, u32[]{:S(2)}) collective-permute-start(f32[1,576]{1,0:T(1,128)S(1)} %reshape.116), channel_id=1, source_target_pairs={{0,16},{1,17},{2,18},{3,19},{4,20},{5,21},{6,22},{7,23},{8,24},{9,... | collective-permute-start | bytes 6920 | tf_op jit(solution)/shard_map/ppermute | solution.py:212
  287.1 8.5 %collective-permute-start.33 = (f32[1,576]{1,0:T(1,128)S(1)}, f32[1,576]{1,0:T(1,128)S(1)}, u32[]{:S(2)}, u32[]{:S(2)}) collective-permute-start(f32[1,576]{1,0:T(1,128)S(1)} %reshape_add_fusion), channel_id=1, source_target_pairs={{0,8},{1,9},{2,10},{3,11},{4,12},{5,13},{6,14},{7,15},{8,0},{9,1},... | collective-permute-start | bytes 6920 | tf_op jit(solution)/shard_map/ppermute | solution.py:212
  294.7 8.1 %collective-permute-start.30 = (bf16[192,576]{0,1:T(8,128)(2,1)S(1)}, bf16[192,576]{0,1:T(8,128)(2,1)S(1)}, u32[]{:S(2)}, u32[]{:S(2)}) collective-permute-start(bf16[192,576]{0,1:T(8,128)(2,1)S(1)} %slice.409), channel_id=1, source_target_pairs={{0,8},{1,9},{2,10},{3,11},{4,12},{5,13},{6,14},{7,15},{8,0},{9,1},... | collective-permute-start | bytes 663560 | tf_op jit(solution)/shard_map/ppermute | solution.py:212
  295.6 3.7 collective-permute-start.34
  297.5 14.5 %copy-start.9 = (f32[512,768]{1,0:T(8,128)S(1)}, f32[512,768]{1,0:T(8,128)}, u32[]{:S(2)}) copy-start(f32[512,768]{1,0:T(8,128)} %copy-done.8) | copy-start | bytes 4718596
  297.5 14.5 %copy-start.27 = (bf16[512,768]{1,0:T(8,128)(2,1)S(1)}, bf16[512,768]{1,0:T(8,128)(2,1)}, u32[]{:S(2)}) copy-start(bf16[512,768]{1,0:T(8,128)(2,1)} %copy-done.26) | copy-start | bytes 2359300
  299.3 29.1 %collective-permute-start.46 = (bf16[768,768]{1,0:T(8,128)(2,1)}, bf16[768,768]{1,0:T(8,128)(2,1)}, u32[]{:S(2)}, u32[]{:S(2)}) collective-permute-start(bf16[768,768]{1,0:T(8,128)(2,1)} %convolution_convert_fusion.2), channel_id=1, source_target_pairs={{0,1},{1,0},{2,3},{3,2},{4,5},{5,4},{6,7},{7,6},{8,9},{9,8},{10,11... | collective-permute-start | bytes 3538952 | tf_op jit(solution)/shard_map/ppermute | solution.py:212
  303.0 8.2 %collective-permute-start.31 = (bf16[96,576]{0,1:T(8,128)(2,1)S(1)}, bf16[96,576]{0,1:T(8,128)(2,1)S(1)}, u32[]{:S(2)}, u32[]{:S(2)}) collective-permute-start(bf16[96,576]{0,1:T(8,128)(2,1)S(1)} %slice.412), channel_id=1, source_target_pairs={{0,16},{1,17},{2,18},{3,19},{4,20},{5,21},{6,22},{7,23},{8,24},{9,... | collective-permute-start | bytes 331784 | tf_op jit(solution)/shard_map/ppermute | solution.py:212
  311.2 51.0 %collective-permute-start.27 = (bf16[1024,768]{1,0:T(8,128)(2,1)}, bf16[1024,768]{1,0:T(8,128)(2,1)}, u32[]{:S(2)}, u32[]{:S(2)}) collective-permute-start(bf16[1024,768]{1,0:T(8,128)(2,1)} %pad_maximum_fusion.1), channel_id=1, source_target_pairs={{0,1},{1,0},{2,3},{3,2},{4,5},{5,4},{6,7},{7,6},{8,9},{9,8},{10,11... | collective-permute-start | bytes 4718600 | tf_op jit(solution)/shard_map/ppermute | solution.py:212
  323.3 35.5 %collective-permute-start.37 = (bf16[768,960]{0,1:T(8,128)(2,1)}, bf16[768,960]{0,1:T(8,128)(2,1)}, u32[]{:S(2)}, u32[]{:S(2)}) collective-permute-start(bf16[768,960]{0,1:T(8,128)(2,1)} %concatenate.156), channel_id=1, source_target_pairs={{0,2},{1,3},{2,0},{3,1},{4,6},{5,7},{6,4},{7,5},{8,10},{9,11},{10,... | collective-permute-start | bytes 4423688 | tf_op jit(solution)/shard_map/ppermute | solution.py:212
  327.9 16.5 %collective-permute-start.49 = (bf16[384,768]{1,0:T(8,128)(2,1)}, bf16[384,768]{1,0:T(8,128)(2,1)}, u32[]{:S(2)}, u32[]{:S(2)}) collective-permute-start(bf16[384,768]{1,0:T(8,128)(2,1)} %pad_maximum_fusion.9), channel_id=1, source_target_pairs={{0,4},{1,5},{2,6},{3,7},{4,0},{5,1},{6,2},{7,3},{8,12},{9,13},{10,... | collective-permute-start | bytes 1769480 | tf_op jit(solution)/shard_map/ppermute | solution.py:212
  332.2 39.2 %collective-permute-start.47 = (bf16[384,768]{1,0:T(8,128)(2,1)}, bf16[384,768]{1,0:T(8,128)(2,1)}, u32[]{:S(2)}, u32[]{:S(2)}) collective-permute-start(bf16[384,768]{1,0:T(8,128)(2,1)} %pad_maximum_fusion.8), channel_id=1, source_target_pairs={{0,4},{1,5},{2,6},{3,7},{4,0},{5,1},{6,2},{7,3},{8,12},{9,13},{10,... | collective-permute-start | bytes 1769480 | tf_op jit(solution)/shard_map/ppermute | solution.py:212
  341.5 17.4 %copy-start.3 = (bf16[768,960]{0,1:T(8,128)(2,1)S(1)}, bf16[768,960]{0,1:T(8,128)(2,1)}, u32[]{:S(2)}) copy-start(bf16[768,960]{0,1:T(8,128)(2,1)} %concatenate.153) | copy-start | bytes 4423684
  346.5 15.7 %copy-start.13 = (bf16[768,576]{1,0:T(8,128)(2,1)S(1)}, bf16[768,576]{1,0:T(8,128)(2,1)}, u32[]{:S(2)}) copy-start(bf16[768,576]{1,0:T(8,128)(2,1)} %copy-done.11) | copy-start | bytes 2654212
  346.5 25.0 %collective-permute-start.50 = (bf16[384,768]{1,0:T(8,128)(2,1)}, bf16[384,768]{1,0:T(8,128)(2,1)}, u32[]{:S(2)}, u32[]{:S(2)}) collective-permute-start(bf16[384,768]{1,0:T(8,128)(2,1)} %add_convert_fusion.7), channel_id=1, source_target_pairs={{0,2},{1,3},{2,0},{3,1},{4,6},{5,7},{6,4},{7,5},{8,10},{9,11},{10,... | collective-permute-start | bytes 1769480 | tf_op jit(solution)/shard_map/ppermute | solution.py:212
  361.8 17.9 %collective-permute-start.38 = (bf16[384,960]{0,1:T(8,128)(2,1)}, bf16[384,960]{0,1:T(8,128)(2,1)}, u32[]{:S(2)}, u32[]{:S(2)}) collective-permute-start(bf16[384,960]{0,1:T(8,128)(2,1)} %slice.299), channel_id=1, source_target_pairs={{0,4},{1,5},{2,6},{3,7},{4,0},{5,1},{6,2},{7,3},{8,12},{9,13},{10,... | collective-permute-start | bytes 2211848 | tf_op jit(solution)/shard_map/ppermute | solution.py:212
  365.3 22.6 %collective-permute-start.28 = (bf16[512,768]{1,0:T(8,128)(2,1)}, bf16[512,768]{1,0:T(8,128)(2,1)}, u32[]{:S(2)}, u32[]{:S(2)}) collective-permute-start(bf16[512,768]{1,0:T(8,128)(2,1)} %add_convert_fusion.5), channel_id=1, source_target_pairs={{0,2},{1,3},{2,0},{3,1},{4,6},{5,7},{6,4},{7,5},{8,10},{9,11},{10,... | collective-permute-start | bytes 2359304 | tf_op jit(solution)/shard_map/ppermute | solution.py:212
  373.2 17.5 %collective-permute-start.51 = (bf16[192,768]{1,0:T(8,128)(2,1)S(1)}, bf16[192,768]{1,0:T(8,128)(2,1)S(1)}, u32[]{:S(2)}, u32[]{:S(2)}) collective-permute-start(bf16[192,768]{1,0:T(8,128)(2,1)S(1)} %slice.408), channel_id=1, source_target_pairs={{0,8},{1,9},{2,10},{3,11},{4,12},{5,13},{6,14},{7,15},{8,0},{9,1},... | collective-permute-start | bytes 884744 | tf_op jit(solution)/shard_map/ppermute | solution.py:212
  381.2 11.5 %collective-permute-start.39 = (bf16[192,960]{0,1:T(8,128)(2,1)S(1)}, bf16[192,960]{0,1:T(8,128)(2,1)S(1)}, u32[]{:S(2)}, u32[]{:S(2)}) collective-permute-start(bf16[192,960]{0,1:T(8,128)(2,1)S(1)} %slice.407), channel_id=1, source_target_pairs={{0,8},{1,9},{2,10},{3,11},{4,12},{5,13},{6,14},{7,15},{8,0},{9,1},... | collective-permute-start | bytes 1105928 | tf_op jit(solution)/shard_map/ppermute | solution.py:212
  390.8 13.2 %collective-permute-start.52 = (bf16[96,768]{1,0:T(8,128)(2,1)S(1)}, bf16[96,768]{1,0:T(8,128)(2,1)S(1)}, u32[]{:S(2)}, u32[]{:S(2)}) collective-permute-start(bf16[96,768]{1,0:T(8,128)(2,1)S(1)} %slice.411), channel_id=1, source_target_pairs={{0,16},{1,17},{2,18},{3,19},{4,20},{5,21},{6,22},{7,23},{8,24},{9,... | collective-permute-start | bytes 442376 | tf_op jit(solution)/shard_map/ppermute | solution.py:212
  392.9 16.3 %collective-permute-start.40 = (bf16[96,960]{0,1:T(8,128)(2,1)S(1)}, bf16[96,960]{0,1:T(8,128)(2,1)S(1)}, u32[]{:S(2)}, u32[]{:S(2)}) collective-permute-start(bf16[96,960]{0,1:T(8,128)(2,1)S(1)} %slice.410), channel_id=1, source_target_pairs={{0,16},{1,17},{2,18},{3,19},{4,20},{5,21},{6,22},{7,23},{8,24},{9,... | collective-permute-start | bytes 552968 | tf_op jit(solution)/shard_map/ppermute | solution.py:212
  (39 other events, 173.3 us)
